TPU v7x, 8 devices: a whole 2x2x1 slice. The times are simulated.
8 devices in a mesh: data: 2 (over z, y), cp: 4 (over x, core).
Axes of the slice: x: 2, y: 2, z: 1, core: 2. Of those that a mesh axis runs over, the one named last changes fastest.
Arguments:
- q: bfloat16 [64, 1024, 12, 128], P('data', 'cp'), parts along dimension 0
- k: bfloat16 [64, 1024, 2, 128], P('data', 'cp'), parts along dimension 0
- v: bfloat16 [64, 1024, 2, 128], P('data', 'cp'), parts along dimension 0
- do: bfloat16 [64, 1024, 12, 128], P('data', 'cp'), parts along dimension 0
- o: bfloat16 [64, 1024, 12, 128], P('data', 'cp'), parts along dimension 0
- lse: float32 [64, 12, 1024], P('data', None, 'cp'), parts along dimension 0
Outputs:
- output 1: bfloat16 [64, 1024, 12, 128], P('data', 'cp'), parts along dimension 0
- output 2: bfloat16 [64, 1024, 2, 128], P('data', 'cp'), parts along dimension 0
- output 3: bfloat16 [64, 1024, 2, 128], P('data', 'cp'), parts along dimension 0
There are 2 independent parts. A program takes and returns all parts, laid end to end along the dimension named above; each array names one.
All inputs are finite; a program needn't handle non-finite values.
Results may differ from a plain program's by a relative error of at most 0.001.
Values are sent between devices in bfloat16 or wider.
A program may use at most 1 GiB of HBM per device.

v0:
```python
import functools
import jax
import jax.numpy as jnp
from jax import lax
from jax.sharding import PartitionSpec as P

F32 = jnp.float32
BF16 = jnp.bfloat16


def _block(q, do, lse, delta, k, v, mask, scale):
    s = jnp.einsum('bhgqd,bhkd->bhgqk', q, k, preferred_element_type=F32) * scale
    x = s - lse[..., None]
    if mask is not None:
        x = jnp.where(mask, x, -jnp.inf)
    p = jnp.exp(x)
    dv = jnp.einsum('bhgqk,bhgqd->bkhd', p.astype(BF16), do, preferred_element_type=F32)
    dp = jnp.einsum('bhgqd,bhkd->bhgqk', do, v, preferred_element_type=F32)
    ds = (p * (dp - delta[..., None])).astype(BF16)
    dq = jnp.einsum('bhgqk,bhkd->bhgqd', ds, k, preferred_element_type=F32)
    dk = jnp.einsum('bhgqk,bhgqd->bkhd', ds, q, preferred_element_type=F32)
    return dq, dk, dv


def _own(q, do, lse, delta, k, v, scale):
    c = q.shape[3] // 2
    tri = jnp.tril(jnp.ones((c, c), dtype=bool))
    mask = jnp.concatenate([tri, jnp.ones((c, c), dtype=bool)], axis=0)
    dq, dk1, dv1 = _block(q, do, lse, delta, k[:, :, :c], v[:, :, :c], mask, scale)
    dq2, dk2, dv2 = _block(q[..., c:, :], do[..., c:, :], lse[..., c:], delta[..., c:], k[:, :, c:], v[:, :, c:], tri, scale)
    return dq.at[..., c:, :].add(dq2), jnp.concatenate([dk1, dk2], 1), jnp.concatenate([dv1, dv2], 1)


def _earlier(q, do, lse, delta, k, v, scale):
    c = q.shape[3] // 2
    dq, dk, dv = _block(q, do, lse, delta, k[:, :, :c], v[:, :, :c], None, scale)
    return dq, jnp.concatenate([dk, jnp.zeros_like(dk)], 1), jnp.concatenate([dv, jnp.zeros_like(dv)], 1)


def _later(q, do, lse, delta, k, v, scale):
    c = q.shape[3] // 2
    dq, dk, dv = _block(q[..., c:, :], do[..., c:, :], lse[..., c:], delta[..., c:], k, v, None, scale)
    return jnp.concatenate([jnp.zeros_like(dq), dq], 3), dk, dv


def _prepare(q, do, o, lse, value_a3):
    b, t, hq, d = q.shape
    g = hq // value_a3
    delta = jnp.sum(do.astype(F32) * o.astype(F32), axis=-1)
    delta = jnp.transpose(delta, (0, 2, 1)).reshape(b, value_a3, g, t)
    qt = jnp.transpose(q.reshape(b, t, value_a3, g, d), (0, 2, 3, 1, 4))
    dot = jnp.transpose(do.reshape(b, t, value_a3, g, d), (0, 2, 3, 1, 4))
    return (qt, dot, lse.reshape(b, value_a3, g, t), delta)


def _heads(x):
    return jnp.transpose(x, (0, 2, 1, 3))


def solution(mesh):
    n = mesh.shape['cp']
    perm = [(r, (r + 1) % n) for r in range(n)]

    def local(q, k, v, do, o, lse):
        b, t, hq, d = q.shape
        scale = d ** -0.5
        i = lax.axis_index('cp')
        args = _prepare(q, do, o, lse, k.shape[2])
        earlier = functools.partial(_earlier, scale=scale)
        later = functools.partial(_later, scale=scale)
        dq, dk, dv = _own(*args, _heads(k), _heads(v), scale)
        kc, vc = k, v
        for step in range(1, n):
            kc, vc, dk, dv = (lax.ppermute(x, 'cp', perm) for x in (kc, vc, dk, dv))
            src = (i - step) % n
            dq_s, dk_s, dv_s = lax.cond(src < i, earlier, later, *args, _heads(kc), _heads(vc))
            dq, dk, dv = dq + dq_s, dk + dk_s, dv + dv_s
        dk, dv = (lax.ppermute(x, 'cp', perm) for x in (dk, dv))
        dq = jnp.transpose(dq * scale, (0, 3, 1, 2, 4)).astype(BF16).reshape(b, t, hq, d)
        return (dq, (dk * scale).astype(BF16), dv.astype(BF16))

    spec = P('data', 'cp')
    return jax.shard_map(local, mesh=mesh, in_specs=(spec, spec, spec, spec, spec, P('data', None, 'cp')),
                         out_specs=(spec, spec, spec), check_vma=False)
```

profile of v0, /device:TPU:0, one launch (start us, length us, event | category | flops | bytes accessed | tf_op | source)
XLA Modules:
  0.0 1662.2 jit_solution(2707474810515944598)
XLA Ops:
  39.7 25.4 %fusion.159 = f32[32,2,6,256,128]{4,3,2,1,0:T(8,128)} fusion(bf16[32,2,6,256,128]{4,3,2,1,0:T(8,128)(2,1)} %bitcast.251, bf16[32,2,256,128]{3,2,1,0:T(8,128)(2,1)} %bitcast.249), kind=kOutput, calls=%fused_computation.147 | convolution fusion | flops 3221225472 | bytes 77594624 | tf_op jit(solution)/shard_map/bhgqd,bhkd->bhgqk/dot_general | solution.py:12
  70.7 23.0 %multiply_convert_fusion.8 = bf16[32,2,6,128,128]{4,3,2,1,0:T(8,128)(2,1)} fusion(f32[32,2,6,128,128]{4,3,2,1,0:T(8,128)} %fusion.143, f32[32,2,6,128]{3,2,1,0:T(8,128)S(1)} %copy.97, f32[32,2,6,128]{3,2,1,0:T(8,128)S(1)} %copy.96, pred[128,128]{1,0:T(8,128)(4,1)S(1)} %iota_compare_fusion, bf16[32,2,6,256,128]{4,3,2,1,0:T(8,128)(2,1)} %bitcast.260, ...), kind=kOutput, calls=%fused_computation.116 | convolution fusion | flops 1648361472 | bytes 52838400 | tf_op jit(solution)/shard_map/bhgqd,bhkd->bhgqk/dot_general | solution.py:18
  106.0 34.3 %multiply_convert_fusion.7 = bf16[32,2,6,256,128]{4,3,2,1,0:T(8,128)(2,1)} fusion(f32[32,2,6,256,128]{4,3,2,1,0:T(8,128)} %fusion.159, f32[32,2,6,256]{3,2,1,0:T(8,128)S(1)} %copy.95, f32[32,2,6,256]{3,2,1,0:T(8,128)S(1)} %copy.92, pred[256,128]{1,0:T(8,128)(4,1)S(1)} %concatenate.38, bf16[32,2,6,256,128]{4,3,2,1,0:T(8,128)(2,1)} %bitcast.261, ...), kind=kOutput, calls=%fused_computation.109 | convolution fusion | flops 3296722944 | bytes 103579648 | tf_op jit(solution)/shard_map/bhgqd,bhkd->bhgqk/dot_general | solution.py:18
  140.3 20.1 %convolution_bitcast_fusion.3 = f32[32,128,2,128]{3,1,2,0:T(8,128)} fusion(bf16[32,2,6,256,128]{4,3,2,1,0:T(8,128)(2,1)} %multiply_convert_fusion.7, bf16[32,2,6,256,128]{4,3,2,1,0:T(8,128)(2,1)} %bitcast.253), kind=kOutput, calls=%fused_computation.140 | convolution fusion | flops 3221225472 | bytes 54525952 | tf_op jit(solution)/shard_map/bhgqk,bhgqd->bkhd/dot_general | solution.py:21
  168.9 33.1 %fusion.150 = f32[32,128,2,128]{3,1,2,0:T(8,128)S(1)} fusion(bf16[32,2,6,256,128]{4,3,2,1,0:T(8,128)(2,1)} %bitcast.262, f32[32,2,6,256,128]{4,3,2,1,0:T(8,128)} %fusion.159, f32[32,2,6,256]{3,2,1,0:T(8,128)S(1)} %copy.92, pred[256,128]{1,0:T(8,128)(4,1)S(1)} %concatenate.38), kind=kOutput, calls=%fused_computation.139 | convolution fusion | flops 3271557120 | bytes 80117760 | tf_op jit(solution)/shard_map/bhgqk,bhgqd->bkhd/dot_general | solution.py:17
  202.1 19.4 %fusion.153 = f32[32,128,2,128]{3,1,2,0:T(8,128)S(1)} fusion(bf16[32,2,6,256,128]{4,3,2,1,0:T(8,128)(2,1)} %bitcast.263, f32[32,2,6,128,128]{4,3,2,1,0:T(8,128)} %fusion.143, f32[32,2,6,128]{3,2,1,0:T(8,128)S(1)} %copy.96, pred[128,128]{1,0:T(8,128)(4,1)S(1)} %iota_compare_fusion), kind=kOutput, calls=%fused_computation.141 | convolution fusion | flops 1635778560 | bytes 42156032 | tf_op jit(solution)/shard_map/bhgqk,bhgqd->bkhd/dot_general | solution.py:17
  227.9 168.9 %collective-permute-done.1 = bf16[32,256,2,128]{3,1,2,0:T(8,128)(2,1)} collective-permute-done((bf16[32,256,2,128]{3,1,2,0:T(8,128)(2,1)}, bf16[32,256,2,128]{3,1,2,0:T(8,128)(2,1)}, u32[]{:S(2)}, u32[]{:S(2)}) %collective-permute-start.1) | collective-permute-done | bytes 4194336 | tf_op jit(solution)/shard_map/ppermute | solution.py:74
  396.8 44.9 %collective-permute-done = bf16[32,256,2,128]{3,1,2,0:T(8,128)(2,1)} collective-permute-done((bf16[32,256,2,128]{3,1,2,0:T(8,128)(2,1)}, bf16[32,256,2,128]{3,1,2,0:T(8,128)(2,1)}, u32[]{:S(2)}, u32[]{:S(2)}) %collective-permute-start) | collective-permute-done | bytes 4194336 | tf_op jit(solution)/shard_map/ppermute | solution.py:74
  441.8 147.8 %conditional.3 = (f32[32,2,6,256,128]{4,3,2,1,0:T(8,128)}, f32[32,256,2,128]{3,1,2,0:T(8,128)}, f32[32,256,2,128]{3,1,2,0:T(8,128)}) conditional(s32[]{:T(128)} %convert_element_type.79, (bf16[32,2,6,256,128]{4,3,2,1,0:T(8,128)(2,1)}, bf16[32,2,256,128]{3,2,1,0:T(8,128)(2,1)}, f32[32,2,6,256]{3,0,2,1:T(8,128)S(1)}, ...), branch_computations={%region_1.2_spmd, %region_2.3_spmd} | conditional | flops 16206790656 | bytes 420872224 | solution.py:76
  442.3 23.3 %fusion.9 = f32[32,2,6,128,256]{4,3,2,1,0:T(8,128)} fusion(bf16[32,2,6,256,128]{4,3,2,1,0:T(8,128)(2,1)} %get-tuple-element.84, bf16[32,2,256,128]{3,2,1,0:T(8,128)(2,1)} %get-tuple-element.85), kind=kOutput, calls=%fused_computation.10 | convolution fusion | flops 3221225472 | bytes 67108864 | tf_op jit(solution)/shard_map/cond/branch_0_fun/bhgqd,bhkd->bhgqk/dot_general | solution.py:12
  465.6 25.9 %fusion.18 = f32[32,256,2,128]{3,1,2,0:T(8,128)} fusion(bf16[32,2,6,256,128]{4,3,2,1,0:T(8,128)(2,1)} %get-tuple-element.87, f32[32,2,6,128,256]{4,3,2,1,0:T(8,128)} %fusion.9, f32[32,2,6,128]{3,2,1,0:T(8,128)S(1)} %slice.121), kind=kOutput, calls=%fused_computation.17 | convolution fusion | flops 3258974208 | bytes 71499776 | tf_op jit(solution)/shard_map/cond/branch_0_fun/bhgqk,bhgqd->bkhd/dot_general | solution.py:17
  491.5 31.9 %multiply_convert_fusion = bf16[32,2,6,128,256]{4,3,2,1,0:T(8,128)(2,1)} fusion(f32[32,2,6,128,256]{4,3,2,1,0:T(8,128)} %fusion.9, f32[32,2,6,128]{3,2,1,0:T(8,128)S(1)} %slice.122, f32[32,2,6,128]{3,2,1,0:T(8,128)S(1)} %slice.121, bf16[32,2,6,256,128]{4,3,2,1,0:T(8,128)(2,1)} %get-tuple-element.87, bf16[32,2,256,128]{3,2,1,0:T(8,128)(2,1)} %get-tuple-element.88), kind=kOutput, calls=%fused_computation | convolution fusion | flops 3284140032 | bytes 92667904 | tf_op jit(solution)/shard_map/cond/branch_0_fun/bhgqd,bhkd->bhgqk/dot_general | solution.py:18
  541.1 17.9 %fusion.12 = f32[32,2,6,128,128]{4,3,2,1,0:T(8,128)} fusion(bf16[32,2,6,128,256]{4,3,2,1,0:T(8,128)(2,1)} %multiply_convert_fusion, bf16[32,2,256,128]{3,2,1,0:T(8,128)(2,1)} %get-tuple-element.85), kind=kOutput, calls=%fused_computation.13 | convolution fusion | flops 3221225472 | bytes 54525952 | tf_op jit(solution)/shard_map/cond/branch_0_fun/bhgqk,bhkd->bhgqd/dot_general | solution.py:20
  559.0 27.4 %concatenate.26 = f32[32,2,6,256,128]{4,3,2,1,0:T(8,128)} pad(f32[32,2,6,128,128]{4,3,2,1,0:T(8,128)} %fusion.12, f32[]{:T(128)} %constant.75.clone), padding=0_0x0_0x0_0x128_0x0_0 | pad | bytes 75497472 | tf_op jit(solution)/shard_map/cond/branch_0_fun/concatenate | solution.py:43
  630.4 211.5 %collective-permute-done.3 = bf16[32,256,2,128]{3,1,2,0:T(8,128)(2,1)} collective-permute-done((bf16[32,256,2,128]{3,1,2,0:T(8,128)(2,1)}, bf16[32,256,2,128]{3,1,2,0:T(8,128)(2,1)}, u32[]{:S(2)}, u32[]{:S(2)}) %collective-permute-start.3) | collective-permute-done | bytes 4194336 | tf_op jit(solution)/shard_map/ppermute | solution.py:74
  842.0 44.9 %collective-permute-done.2 = bf16[32,256,2,128]{3,1,2,0:T(8,128)(2,1)} collective-permute-done((bf16[32,256,2,128]{3,1,2,0:T(8,128)(2,1)}, bf16[32,256,2,128]{3,1,2,0:T(8,128)(2,1)}, u32[]{:S(2)}, u32[]{:S(2)}) %collective-permute-start.2) | collective-permute-done | bytes 4194336 | tf_op jit(solution)/shard_map/ppermute | solution.py:74
  886.9 149.3 %conditional.4 = (f32[32,2,6,256,128]{4,3,2,1,0:T(8,128)}, f32[32,256,2,128]{3,1,2,0:T(8,128)}, f32[32,256,2,128]{3,1,2,0:T(8,128)}) conditional(s32[]{:T(128)} %convert_element_type.80, (bf16[32,2,6,256,128]{4,3,2,1,0:T(8,128)(2,1)}, bf16[32,2,256,128]{3,2,1,0:T(8,128)(2,1)}, f32[32,2,6,256]{3,0,2,1:T(8,128)S(1)}, ...), branch_computations={%region_3.4_spmd, %region_4.5_spmd} | conditional | flops 16206790656 | bytes 420872224 | solution.py:76
  887.7 23.0 %fusion.50 = f32[32,2,6,128,256]{4,3,2,1,0:T(8,128)} fusion(bf16[32,2,6,256,128]{4,3,2,1,0:T(8,128)(2,1)} %get-tuple-element.96, bf16[32,2,256,128]{3,2,1,0:T(8,128)(2,1)} %get-tuple-element.97), kind=kOutput, calls=%fused_computation.46 | convolution fusion | flops 3221225472 | bytes 67108864 | tf_op jit(solution)/shard_map/cond/branch_0_fun/bhgqd,bhkd->bhgqk/dot_general | solution.py:12
  910.7 25.9 %fusion.59 = f32[32,256,2,128]{3,1,2,0:T(8,128)} fusion(bf16[32,2,6,256,128]{4,3,2,1,0:T(8,128)(2,1)} %get-tuple-element.99, f32[32,2,6,128,256]{4,3,2,1,0:T(8,128)} %fusion.50, f32[32,2,6,128]{3,2,1,0:T(8,128)S(1)} %slice.123), kind=kOutput, calls=%fused_computation.53 | convolution fusion | flops 3258974208 | bytes 71499776 | tf_op jit(solution)/shard_map/cond/branch_0_fun/bhgqk,bhgqd->bkhd/dot_general | solution.py:17
  936.6 31.9 %multiply_convert_fusion.2 = bf16[32,2,6,128,256]{4,3,2,1,0:T(8,128)(2,1)} fusion(f32[32,2,6,128,256]{4,3,2,1,0:T(8,128)} %fusion.50, f32[32,2,6,128]{3,2,1,0:T(8,128)S(1)} %slice.124, f32[32,2,6,128]{3,2,1,0:T(8,128)S(1)} %slice.123, bf16[32,2,6,256,128]{4,3,2,1,0:T(8,128)(2,1)} %get-tuple-element.99, bf16[32,2,256,128]{3,2,1,0:T(8,128)(2,1)} %get-tuple-element.100), kind=kOutput, calls=%fused_computation.36 | convolution fusion | flops 3284140032 | bytes 92667904 | tf_op jit(solution)/shard_map/cond/branch_0_fun/bhgqd,bhkd->bhgqk/dot_general | solution.py:18
  1004.2 27.3 %concatenate.29 = f32[32,2,6,256,128]{4,3,2,1,0:T(8,128)} pad(f32[32,2,6,128,128]{4,3,2,1,0:T(8,128)} %fusion.53, f32[]{:T(128)} %constant.79.clone), padding=0_0x0_0x0_0x128_0x0_0 | pad | bytes 75497472 | tf_op jit(solution)/shard_map/cond/branch_0_fun/concatenate | solution.py:43
  1078.0 25.5 %fusion.158 = f32[32,2,6,256,128]{4,3,2,1,0:T(8,128)} fusion(bf16[32,2,6,256,128]{4,3,2,1,0:T(8,128)(2,1)} %multiply_convert_fusion.7, bf16[32,2,256,128]{3,2,1,0:T(8,128)(2,1)} %bitcast.249), kind=kOutput, calls=%fused_computation.146 | convolution fusion | flops 3221225472 | bytes 77594624 | tf_op jit(solution)/shard_map/bhgqk,bhkd->bhgqd/dot_general | solution.py:20
  1103.5 183.6 %collective-permute-done.5 = bf16[32,256,2,128]{3,1,2,0:T(8,128)(2,1)} collective-permute-done((bf16[32,256,2,128]{3,1,2,0:T(8,128)(2,1)}, bf16[32,256,2,128]{3,1,2,0:T(8,128)(2,1)}, u32[]{:S(2)}, u32[]{:S(2)}) %collective-permute-start.5) | collective-permute-done | bytes 4194336 | tf_op jit(solution)/shard_map/ppermute | solution.py:74
  1287.0 44.9 %collective-permute-done.4 = bf16[32,256,2,128]{3,1,2,0:T(8,128)(2,1)} collective-permute-done((bf16[32,256,2,128]{3,1,2,0:T(8,128)(2,1)}, bf16[32,256,2,128]{3,1,2,0:T(8,128)(2,1)}, u32[]{:S(2)}, u32[]{:S(2)}) %collective-permute-start.4) | collective-permute-done | bytes 4194336 | tf_op jit(solution)/shard_map/ppermute | solution.py:74
  1332.0 149.8 %conditional.5 = (f32[32,2,6,256,128]{4,3,2,1,0:T(8,128)}, f32[32,256,2,128]{3,1,2,0:T(8,128)}, f32[32,256,2,128]{3,1,2,0:T(8,128)}) conditional(s32[]{:T(128)} %convert_element_type.81, (bf16[32,2,6,256,128]{4,3,2,1,0:T(8,128)(2,1)}, bf16[32,2,256,128]{3,2,1,0:T(8,128)(2,1)}, f32[32,2,6,256]{3,0,2,1:T(8,128)S(1)}, ...), branch_computations={%region_5.6_spmd, %region_6.7_spmd} | conditional | flops 16206790656 | bytes 420872224 | solution.py:76
  1332.7 23.0 %fusion.91 = f32[32,2,6,128,256]{4,3,2,1,0:T(8,128)} fusion(bf16[32,2,6,256,128]{4,3,2,1,0:T(8,128)(2,1)} %get-tuple-element.108, bf16[32,2,256,128]{3,2,1,0:T(8,128)(2,1)} %get-tuple-element.109), kind=kOutput, calls=%fused_computation.82 | convolution fusion | flops 3221225472 | bytes 67108864 | tf_op jit(solution)/shard_map/cond/branch_0_fun/bhgqd,bhkd->bhgqk/dot_general | solution.py:12
  1355.8 25.9 %fusion.100 = f32[32,256,2,128]{3,1,2,0:T(8,128)} fusion(bf16[32,2,6,256,128]{4,3,2,1,0:T(8,128)(2,1)} %get-tuple-element.111, f32[32,2,6,128,256]{4,3,2,1,0:T(8,128)} %fusion.91, f32[32,2,6,128]{3,2,1,0:T(8,128)S(1)} %slice.125), kind=kOutput, calls=%fused_computation.89 | convolution fusion | flops 3258974208 | bytes 71499776 | tf_op jit(solution)/shard_map/cond/branch_0_fun/bhgqk,bhgqd->bkhd/dot_general | solution.py:17
  1381.7 31.9 %multiply_convert_fusion.4 = bf16[32,2,6,128,256]{4,3,2,1,0:T(8,128)(2,1)} fusion(f32[32,2,6,128,256]{4,3,2,1,0:T(8,128)} %fusion.91, f32[32,2,6,128]{3,2,1,0:T(8,128)S(1)} %slice.126, f32[32,2,6,128]{3,2,1,0:T(8,128)S(1)} %slice.125, bf16[32,2,6,256,128]{4,3,2,1,0:T(8,128)(2,1)} %get-tuple-element.111, bf16[32,2,256,128]{3,2,1,0:T(8,128)(2,1)} %get-tuple-element.112), kind=kOutput, calls=%fused_computation.72 | convolution fusion | flops 3284140032 | bytes 92667904 | tf_op jit(solution)/shard_map/cond/branch_0_fun/bhgqd,bhkd->bhgqk/dot_general | solution.py:18
  1449.2 27.4 %concatenate.32 = f32[32,2,6,256,128]{4,3,2,1,0:T(8,128)} pad(f32[32,2,6,128,128]{4,3,2,1,0:T(8,128)} %fusion.94, f32[]{:T(128)} %constant.83.clone), padding=0_0x0_0x0_0x128_0x0_0 | pad | bytes 75497472 | tf_op jit(solution)/shard_map/cond/branch_0_fun/concatenate | solution.py:43
  1498.0 23.2 %fusion.126 = f32[32,2,6,256,128]{4,3,2,1,0:T(8,128)} fusion(f32[32,2,6,256,128]{4,3,2,1,0:T(8,128)} %fusion.158, bf16[32,2,6,128,128]{4,3,2,1,0:T(8,128)(2,1)} %multiply_convert_fusion.8, bf16[32,2,256,128]{3,2,1,0:T(8,128)(2,1)} %bitcast.249), kind=kOutput, calls=%fused_computation.115 | convolution fusion | flops 1616904192 | bytes 65011712 | tf_op jit(solution)/shard_map/bhgqk,bhkd->bhgqd/dot_general | solution.py:20
  1531.3 70.1 %multiply_convert_fusion.6 = bf16[32,2,6,256,128]{4,3,2,1,0:T(8,128)(2,1)} fusion(f32[32,2,6,256,128]{4,3,2,1,0:T(8,128)} %get-tuple-element.134, f32[32,2,6,256,128]{4,3,2,1,0:T(8,128)} %get-tuple-element.133, f32[32,2,6,256,128]{4,3,2,1,0:T(8,128)} %fusion.126, f32[32,2,6,256,128]{4,3,2,1,0:T(8,128)} %get-tuple-element.132), kind=kLoop, calls=%fused_computation.108 | loop fusion | flops 62914560 | bytes 226492416 | tf_op jit(solution)/shard_map/convert_element_type | solution.py:79
  1601.4 40.8 %collective-permute-done.13 = bf16[32,256,2,128]{3,1,2,0:T(8,128)(2,1)} collective-permute-done((bf16[32,256,2,128]{3,1,2,0:T(8,128)(2,1)S(1)}, bf16[32,256,2,128]{3,1,2,0:T(8,128)(2,1)}, u32[]{:S(2)}, u32[]{:S(2)}) %collective-permute-start.13) | collective-permute-done | bytes 4194336 | tf_op jit(solution)/shard_map/ppermute | solution.py:78
  (73 shorter events, 290.6 us)
Async XLA Ops:
  19.7 20.0 %copy-start.1 = (f32[32,256,12]{1,2,0:T(8,128)}, f32[32,256,12]{1,2,0:T(8,128)S(1)}, u32[]{:S(2)}) copy-start(f32[32,256,12]{1,2,0:T(8,128)S(1)} %multiply_reduce_fusion) | copy-start | bytes 1179652
  20.0 0.8 copy-start.3
  168.1 421.5 %collective-permute-start.6 = (f32[32,256,2,128]{3,1,2,0:T(8,128)}, f32[32,256,2,128]{3,1,2,0:T(8,128)}, u32[]{:S(2)}, u32[]{:S(2)}) collective-permute-start(f32[32,256,2,128]{3,1,2,0:T(8,128)} %pad_maximum_fusion), channel_id=1, source_target_pairs={{0,1},{1,2},{2,3},{3,0},{4,5},{5,6},{6,7},{7,4}} | collective-permute-start | bytes 25165832 | tf_op jit(solution)/shard_map/ppermute | solution.py:74
  202.1 239.7 %copy-start = (f32[32,12,256]{2,0,1:T(8,128)S(1)}, f32[32,12,256]{2,0,1:T(8,128)}, u32[]{:S(2)}) copy-start(f32[32,12,256]{2,0,1:T(8,128)} %param.19) | copy-start | bytes 1179652
  202.1 239.7 %copy-start.2 = (f32[32,256,12]{1,2,0:T(8,128)S(1)}, f32[32,256,12]{1,2,0:T(8,128)}, u32[]{:S(2)}) copy-start(f32[32,256,12]{1,2,0:T(8,128)} %copy-done.1) | copy-start | bytes 1179652
  202.1 239.6 %copy-start.4 = (f32[32,12,256]{2,0,1:T(8,128)S(1)}, f32[32,12,256]{2,0,1:T(8,128)}, u32[]{:S(2)}) copy-start(f32[32,12,256]{2,0,1:T(8,128)} %copy-done.3) | copy-start | bytes 1179652
  225.3 391.4 %collective-permute-start.10 = (f32[32,256,2,128]{3,1,2,0:T(8,128)}, f32[32,256,2,128]{3,1,2,0:T(8,128)}, u32[]{:S(2)}, u32[]{:S(2)}) collective-permute-start(f32[32,256,2,128]{3,1,2,0:T(8,128)} %pad_maximum_fusion.1), channel_id=1, source_target_pairs={{0,1},{1,2},{2,3},{3,0},{4,5},{5,6},{6,7},{7,4}} | collective-permute-start | bytes 25165832 | tf_op jit(solution)/shard_map/ppermute | solution.py:74
  227.9 168.9 %collective-permute-start.1 = (bf16[32,256,2,128]{3,1,2,0:T(8,128)(2,1)}, bf16[32,256,2,128]{3,1,2,0:T(8,128)(2,1)}, u32[]{:S(2)}, u32[]{:S(2)}) collective-permute-start(bf16[32,256,2,128]{3,1,2,0:T(8,128)(2,1)} %copy.167), channel_id=1, source_target_pairs={{0,1},{1,2},{2,3},{3,0},{4,5},{5,6},{6,7},{7,4}} | collective-permute-start | bytes 12582920 | tf_op jit(solution)/shard_map/ppermute | solution.py:74
  227.9 213.8 %collective-permute-start = (bf16[32,256,2,128]{3,1,2,0:T(8,128)(2,1)}, bf16[32,256,2,128]{3,1,2,0:T(8,128)(2,1)}, u32[]{:S(2)}, u32[]{:S(2)}) collective-permute-start(bf16[32,256,2,128]{3,1,2,0:T(8,128)(2,1)} %copy.168), channel_id=1, source_target_pairs={{0,1},{1,2},{2,3},{3,0},{4,5},{5,6},{6,7},{7,4}} | collective-permute-start | bytes 12582920 | tf_op jit(solution)/shard_map/ppermute | solution.py:74
  600.7 435.5 %collective-permute-start.7 = (f32[32,256,2,128]{3,1,2,0:T(8,128)}, f32[32,256,2,128]{3,1,2,0:T(8,128)}, u32[]{:S(2)}, u32[]{:S(2)}) collective-permute-start(f32[32,256,2,128]{3,1,2,0:T(8,128)} %add.72), channel_id=1, source_target_pairs={{0,1},{1,2},{2,3},{3,0},{4,5},{5,6},{6,7},{7,4}} | collective-permute-start | bytes 25165832 | tf_op jit(solution)/shard_map/ppermute | solution.py:74
  627.9 422.0 %collective-permute-start.11 = (f32[32,256,2,128]{3,1,2,0:T(8,128)}, f32[32,256,2,128]{3,1,2,0:T(8,128)}, u32[]{:S(2)}, u32[]{:S(2)}) collective-permute-start(f32[32,256,2,128]{3,1,2,0:T(8,128)} %add.75), channel_id=1, source_target_pairs={{0,1},{1,2},{2,3},{3,0},{4,5},{5,6},{6,7},{7,4}} | collective-permute-start | bytes 25165832 | tf_op jit(solution)/shard_map/ppermute | solution.py:74
  630.4 211.6 %collective-permute-start.3 = (bf16[32,256,2,128]{3,1,2,0:T(8,128)(2,1)}, bf16[32,256,2,128]{3,1,2,0:T(8,128)(2,1)}, u32[]{:S(2)}, u32[]{:S(2)}) collective-permute-start(bf16[32,256,2,128]{3,1,2,0:T(8,128)(2,1)} %collective-permute-done.1), channel_id=1, source_target_pairs={{0,1},{1,2},{2,3},{3,0},{4,5},{5,6},{6,7},{7,4}} | collective-permute-start | bytes 12582920 | tf_op jit(solution)/shard_map/ppermute | solution.py:74
  630.4 256.5 %collective-permute-start.2 = (bf16[32,256,2,128]{3,1,2,0:T(8,128)(2,1)}, bf16[32,256,2,128]{3,1,2,0:T(8,128)(2,1)}, u32[]{:S(2)}, u32[]{:S(2)}) collective-permute-start(bf16[32,256,2,128]{3,1,2,0:T(8,128)(2,1)} %collective-permute-done), channel_id=1, source_target_pairs={{0,1},{1,2},{2,3},{3,0},{4,5},{5,6},{6,7},{7,4}} | collective-permute-start | bytes 12582920 | tf_op jit(solution)/shard_map/ppermute | solution.py:74
  1047.4 434.4 %collective-permute-start.8 = (f32[32,256,2,128]{3,1,2,0:T(8,128)}, f32[32,256,2,128]{3,1,2,0:T(8,128)}, u32[]{:S(2)}, u32[]{:S(2)}) collective-permute-start(f32[32,256,2,128]{3,1,2,0:T(8,128)} %add.73), channel_id=1, source_target_pairs={{0,1},{1,2},{2,3},{3,0},{4,5},{5,6},{6,7},{7,4}} | collective-permute-start | bytes 25165832 | tf_op jit(solution)/shard_map/ppermute | solution.py:74
  1061.0 460.2 %collective-permute-start.12 = (f32[32,256,2,128]{3,1,2,0:T(8,128)}, f32[32,256,2,128]{3,1,2,0:T(8,128)}, u32[]{:S(2)}, u32[]{:S(2)}) collective-permute-start(f32[32,256,2,128]{3,1,2,0:T(8,128)} %add.76), channel_id=1, source_target_pairs={{0,1},{1,2},{2,3},{3,0},{4,5},{5,6},{6,7},{7,4}} | collective-permute-start | bytes 25165832 | tf_op jit(solution)/shard_map/ppermute | solution.py:74
  1077.9 209.1 %collective-permute-start.5 = (bf16[32,256,2,128]{3,1,2,0:T(8,128)(2,1)}, bf16[32,256,2,128]{3,1,2,0:T(8,128)(2,1)}, u32[]{:S(2)}, u32[]{:S(2)}) collective-permute-start(bf16[32,256,2,128]{3,1,2,0:T(8,128)(2,1)} %collective-permute-done.3), channel_id=1, source_target_pairs={{0,1},{1,2},{2,3},{3,0},{4,5},{5,6},{6,7},{7,4}} | collective-permute-start | bytes 12582920 | tf_op jit(solution)/shard_map/ppermute | solution.py:74
  1077.9 254.0 %collective-permute-start.4 = (bf16[32,256,2,128]{3,1,2,0:T(8,128)(2,1)}, bf16[32,256,2,128]{3,1,2,0:T(8,128)(2,1)}, u32[]{:S(2)}, u32[]{:S(2)}) collective-permute-start(bf16[32,256,2,128]{3,1,2,0:T(8,128)(2,1)} %collective-permute-done.2), channel_id=1, source_target_pairs={{0,1},{1,2},{2,3},{3,0},{4,5},{5,6},{6,7},{7,4}} | collective-permute-start | bytes 12582920 | tf_op jit(solution)/shard_map/ppermute | solution.py:74
  1493.1 157.7 %collective-permute-start.9 = (f32[32,256,2,128]{3,1,2,0:T(8,128)}, f32[32,256,2,128]{3,1,2,0:T(8,128)}, u32[]{:S(2)}, u32[]{:S(2)}) collective-permute-start(f32[32,256,2,128]{3,1,2,0:T(8,128)} %add.74), channel_id=1, source_target_pairs={{0,1},{1,2},{2,3},{3,0},{4,5},{5,6},{6,7},{7,4}} | collective-permute-start | bytes 25165832 | tf_op jit(solution)/shard_map/ppermute | solution.py:78
  1528.8 113.5 %collective-permute-start.13 = (bf16[32,256,2,128]{3,1,2,0:T(8,128)(2,1)S(1)}, bf16[32,256,2,128]{3,1,2,0:T(8,128)(2,1)}, u32[]{:S(2)}, u32[]{:S(2)}) collective-permute-start(bf16[32,256,2,128]{3,1,2,0:T(8,128)(2,1)S(1)} %add.77), channel_id=1, source_target_pairs={{0,1},{1,2},{2,3},{3,0},{4,5},{5,6},{6,7},{7,4}} | collective-permute-start | bytes 12582920 | tf_op jit(solution)/shard_map/ppermute | solution.py:78
where the time goes:
time: 1670 us; the launch traced here: 1660 us
  waiting for transfers between devices  740 us (44%)
  matrix products  579 us (35%)
  other arithmetic  166 us (10%)
  local copies, waits for them, and re-layouts  113 us (7%)
  starting transfers between devices  48.9 us (3%)
    ppermute x12, waiting for transfers between devices, local(): kc, vc, dk, dv = (lax.ppermute(x, 'cp', perm) for x in (kc, vc, dk, dv))  699 us
    dot_general x5, matrix products, _block(): dp = jnp.einsum('bhgqd,bhkd->bhgqk', do, v, preferred_element_type=F32)  153 us
    dot_general x5, matrix products, _block(): jnp.einsum('bhgqk,bhgqd->bkhd', p.astype(BF16), do, preferred_element_typ...  130 us
    dot_general x5, matrix products, _block(): jnp.einsum('bhgqd,bhkd->bhgqk', q, k, preferred_element_type=F32) * scale  108 us
    dot_general x5, matrix products, _block(): dq = jnp.einsum('bhgqk,bhkd->bhgqd', ds, k, preferred_element_type=F32)  102 us
    dot_general x5, matrix products, _block(): dk = jnp.einsum('bhgqk,bhgqd->bkhd', ds, q, preferred_element_type=F32)  85.3 us
    concatenate x3, local copies, waits for them, and re-layouts, _later(): return (jnp.concatenate([jnp.zeros_like(dq), dq], 3), dk, dv)  82.1 us
    convert_element_type x1, other arithmetic, local(): jnp.transpose(dq * scale, (0, 3, 1, 2, 4)).astype(BF16).reshape(b, t, hq, d)  70.1 us
  transfers between devices with their start and end apart: 14, of which 7 were waited for; matrix products, arithmetic and copies ran while one was open for 41% of the time, Pallas kernels for 0%

commit v1 on v0

v1 whole, which is shorter than its diff:
```python
import functools
import jax
import jax.numpy as jnp
from jax import lax
from jax.experimental import pallas as pl
from jax.experimental.pallas import tpu as pltpu
from jax.sharding import PartitionSpec as P

F32 = jnp.float32
BF16 = jnp.bfloat16
MESH = pl.DeviceIdType.MESH

C = 128
GB = 4
NP = 4
LAG = 7
NO = 8

OWN, PARTNER, PEER, DIAG = 0, 1, 2, 3


def _dot(a, b):
    return lax.dot_general(a, b, (((1,), (0,)), ((), ())), preferred_element_type=F32)


def _kernel(nb, hkv, grp, scale,
            q_ref, do_ref, o_ref, lse_ref, k_hbm, v_hbm,
            dq_ref, dk_ref, dv_ref, rl_hbm,
            kl, vl, acc, dl, ps, osum, buf, qt, dot_, dqt, lse_s, del_s,
            loc_sem, xs_sem, xr_sem, es_sem, er_sem, fs_sem, fr_sem,
            ds_sem, dr_sem, ps_sem, pr_sem, buf_sem, credit):
    i = pl.program_id(0)
    r = lax.axis_index('cp')
    chip = r // 2
    odd = lax.rem(r, 2)
    peer = r + 1 - 2 * odd
    partner = lax.rem(r + 2, 4)
    ng = nb // GB
    rows = grp * C

    def kv(which):
        return (k_hbm, kl) if which == 0 else (v_hbm, vl)

    def local_copy(j, w):
        src, dst = kv(w)
        b = pl.ds(j * GB, GB)
        return pltpu.make_async_copy(src.at[b], dst.at[b, OWN], loc_sem.at[j, w])

    def peer_copy(j, w):
        src, dst = kv(w)
        b = pl.ds(j * GB, GB)
        return pltpu.make_async_remote_copy(src.at[b], dst.at[b, PEER], es_sem.at[j, w], er_sem.at[j, w],
                                            device_id={'cp': peer}, device_id_type=MESH)

    def x_copy(j, w, full):
        src, dst = kv(w)
        b = pl.ds(j * GB, GB)
        t = pl.ds(0, 2 * C if full else C)
        return pltpu.make_async_remote_copy(src.at[b, :, t], dst.at[b, PARTNER, :, t], xs_sem.at[j, w], xr_sem.at[j, w],
                                            device_id={'cp': partner}, device_id_type=MESH)

    def fwd_copy(j, w, full):
        _, dst = kv(w)
        b = pl.ds(j * GB, GB)
        t = pl.ds(0, 2 * C if full else C)
        return pltpu.make_async_remote_copy(dst.at[b, PARTNER, :, t], dst.at[b, DIAG, :, t], fs_sem.at[j, w], fr_sem.at[j, w],
                                            device_id={'cp': peer}, device_id_type=MESH)

    def part_copy(m):
        s = lax.rem(m, 2)
        return pltpu.make_async_remote_copy(acc.at[s, pl.ds(4, 4)], dl.at[s], ds_sem.at[s], dr_sem.at[s],
                                            device_id={'cp': peer}, device_id_type=MESH)

    def sum_copy(m, full):
        s = lax.rem(m, NP)
        n = pl.ds(0, 2 if full else 1)
        return pltpu.make_async_remote_copy(ps.at[s, n], rl_hbm.at[m, n], ps_sem.at[s], pr_sem.at[m],
                                            device_id={'cp': partner}, device_id_type=MESH)

    def forward(j):
        for c, full in ((0, True), (1, False)):
            @pl.when(chip == c)
            def _():
                for w in range(2):
                    x_copy(j, w, full).wait_recv()
                    fwd_copy(j, w, full).start()

    @pl.when(i == 0)
    def _():
        barrier = pltpu.get_barrier_semaphore()
        for other in (peer, partner):
            pl.semaphore_signal(barrier, inc=1, device_id={'cp': other}, device_id_type=MESH)
        pl.semaphore_wait(barrier, 2)

        @pl.loop(0, ng)
        def _(j):
            for c, full in ((0, False), (1, True)):
                @pl.when(chip == c)
                def _():
                    for w in range(2):
                        x_copy(j, w, full).start()
            for w in range(2):
                local_copy(j, w).start()
                peer_copy(j, w).start()
        buf[...] = jnp.zeros_like(buf)
        forward(0)

    @pl.when(i < nb)
    def _():
        b = i
        slot = lax.rem(i, 2)
        j = i // GB

        @pl.when(lax.rem(i, GB) == 0)
        def _():
            for w in range(2):
                local_copy(j, w).wait()
                peer_copy(j, w).wait_recv()
            for c, full in ((0, True), (1, False)):
                @pl.when(chip == c)
                def _():
                    for w in range(2):
                        fwd_copy(j, w, full).wait_recv()

        @pl.when((lax.rem(i, GB) == GB // 2) & (i < nb - GB))
        def _():
            forward(j + 1)

        acc[slot] = jnp.zeros(acc.shape[1:], F32)
        dqt[...] = jnp.zeros_like(dqt)
        row = lax.rem(i, 8)
        for g in range(hkv):
            for hh in range(grp):
                h = g * grp + hh
                lanes = pl.ds(hh * C, C)
                lse_row = lse_ref[h, pl.ds(row, 1), :]
                for sg in range(2):
                    tok = pl.ds(sg * C, C)
                    dob = do_ref[0, h, tok, :]
                    qt[sg, g, :, lanes] = q_ref[0, h, tok, :].T
                    dot_[sg, g, :, lanes] = dob.T
                    prod = dob.astype(F32) * o_ref[0, h, tok, :].astype(F32)
                    del_s[sg, g, :, lanes] = jnp.sum(prod.T, axis=0, keepdims=True)
                    lse_s[sg, g, :, lanes] = lse_row[:, sg * C:(sg + 1) * C]

        def pair(qs, ks, shift):
            sec, half = ks // 2, lax.rem(ks, 2)
            keys = pl.ds(pl.multiple_of(half * C, C), C)
            toks = pl.ds(pl.multiple_of(qs * C, C), C)
            for g in range(hkv):
                k = kl[b, sec, g, keys, :]
                v = vl[b, sec, g, keys, :]
                heads = pl.ds(g * grp, grp)
                s = _dot(k, qt[qs, g])
                p = jnp.exp(s * scale - lse_s[qs, g])
                if shift is not None:
                    ki = lax.broadcasted_iota(jnp.int32, (C, rows), 0)
                    qi = lax.bitwise_and(lax.broadcasted_iota(jnp.int32, (C, rows), 1), C - 1)
                    p = jnp.where(ki <= qi + shift, p, 0.0)
                dp = _dot(v, dot_[qs, g])
                ds = (p * (dp - del_s[qs, g])).astype(BF16)
                acc[slot, ks, g, 1] += _dot(p.astype(BF16), do_ref[0, heads, toks, :].reshape(rows, C))
                acc[slot, ks, g, 0] += _dot(ds, q_ref[0, heads, toks, :].reshape(rows, C))
                dqt[qs, g] += _dot(k.T, ds)

        @pl.loop(0, 3)
        def _(t):
            pair((t + 1) // 2, t // 2, C * lax.rem(t, 2))

        @pl.loop(0, 2)
        def _(t):
            pair(1 - odd * (1 - t), 4 + t * (1 - odd), None)

        @pl.loop(0, 4)
        def _(t):
            u = (1 - chip) * t + chip * 2 * (t // 2)
            pair((1 - chip) + chip * lax.rem(t, 2), 2 + lax.rem(u, 2) + 4 * (u // 2), None)

        for g in range(hkv):
            for hh in range(grp):
                for sg in range(2):
                    x = dqt[sg, g, :, pl.ds(hh * C, C)].T
                    dq_ref[0, g * grp + hh, pl.ds(sg * C, C), :] = (x * scale).astype(BF16)

        @pl.when(i >= 2)
        def _():
            pl.semaphore_wait(credit, 1)
        part_copy(i).start()

    @pl.when((i >= 1) & (i <= nb))
    def _():
        m = i - 1
        s = lax.rem(m, 2)
        s4 = lax.rem(m, NP)
        copy = part_copy(m)
        copy.wait_send()
        copy.wait_recv()
        osum[lax.rem(m, NO)] = acc[s, pl.ds(0, 2)] + dl[s, pl.ds(0, 2)]
        for c, full in ((0, True), (1, False)):
            @pl.when((chip == c) & (m >= NP))
            def _():
                sum_copy(m - NP, full).wait_send()
        ps[s4] = acc[s, pl.ds(2, 2)] + dl[s, pl.ds(2, 2)]

        @pl.when(m < nb - 2)
        def _():
            pl.semaphore_signal(credit, inc=1, device_id={'cp': peer}, device_id_type=MESH)
        for c, full in ((0, True), (1, False)):
            @pl.when(chip == c)
            def _():
                sum_copy(m, full).start()

    @pl.when(i >= LAG)
    def _():
        m = i - LAG
        for c, full in ((0, False), (1, True)):
            @pl.when(chip == c)
            def _():
                sum_copy(m, full).wait_recv()
                n = pl.ds(0, 2 if full else 1)
                copy = pltpu.make_async_copy(rl_hbm.at[m, n], buf.at[n], buf_sem)
                copy.start()
                copy.wait()
        so = lax.rem(m, NO)
        for sg in range(2):
            for g in range(hkv):
                tok = pl.ds(sg * C, C)
                dk_ref[0, g, tok, :] = ((osum[so, sg, g, 0] + buf[sg, g, 0]) * scale).astype(BF16)
                dv_ref[0, g, tok, :] = (osum[so, sg, g, 1] + buf[sg, g, 1]).astype(BF16)

    @pl.when(i == nb + LAG - 1)
    def _():
        for c, full in ((0, True), (1, False)):
            @pl.when(chip == c)
            def _():
                for m in range(nb - NP, nb):
                    sum_copy(m, full).wait_send()

        @pl.loop(0, ng)
        def _(j):
            for w in range(2):
                peer_copy(j, w).wait_send()
            for c, full in ((0, False), (1, True)):
                @pl.when(chip == c)
                def _():
                    for w in range(2):
                        x_copy(j, w, full).wait_send()
                        fwd_copy(j, w, not full).wait_send()


def solution(mesh):
    def local(q, k, v, do, o, lse):
        b, t, hq, d = q.shape
        hkv = k.shape[2]
        grp = hq // hkv
        scale = d ** -0.5
        ng = b // GB
        heads = lambda x: jnp.transpose(x, (0, 2, 1, 3))
        q, do, o, k, v = (heads(x) for x in (q, do, o, k, v))
        lse = jnp.transpose(lse, (1, 0, 2))

        last = b - 1
        big = pl.BlockSpec((1, hq, t, d), lambda i: (jnp.minimum(i, last), 0, 0, 0))
        out = pl.BlockSpec((1, hkv, t, d), lambda i: (jnp.maximum(i - LAG, 0), 0, 0, 0))
        anyspec = pl.BlockSpec(memory_space=pl.ANY)
        dma = pltpu.SemaphoreType.DMA
        flops = 9 * b * hq * 5 * 2 * C * C * d
        dq, dk, dv, _ = pl.pallas_call(
            functools.partial(_kernel, b, hkv, grp, scale),
            grid=(b + LAG,),
            in_specs=[big, big, big,
                      pl.BlockSpec((hq, 8, t), lambda i: (0, jnp.minimum(i, last) // 8, 0)),
                      anyspec, anyspec],
            out_specs=[big, out, out, anyspec],
            out_shape=[jax.ShapeDtypeStruct((b, hq, t, d), BF16),
                       jax.ShapeDtypeStruct((b, hkv, t, d), BF16),
                       jax.ShapeDtypeStruct((b, hkv, t, d), BF16),
                       jax.ShapeDtypeStruct((b, 2, hkv, 2, C, d), F32)],
            scratch_shapes=[
                pltpu.VMEM((b, 4, hkv, t, d), BF16),
                pltpu.VMEM((b, 4, hkv, t, d), BF16),
                pltpu.VMEM((2, 8, hkv, 2, C, d), F32),
                pltpu.VMEM((2, 4, hkv, 2, C, d), F32),
                pltpu.VMEM((NP, 2, hkv, 2, C, d), F32),
                pltpu.VMEM((NO, 2, hkv, 2, C, d), F32),
                pltpu.VMEM((2, hkv, 2, C, d), F32),
                pltpu.VMEM((2, hkv, d, grp * C), BF16),
                pltpu.VMEM((2, hkv, d, grp * C), BF16),
                pltpu.VMEM((2, hkv, d, grp * C), F32),
                pltpu.VMEM((2, hkv, 1, grp * C), F32),
                pltpu.VMEM((2, hkv, 1, grp * C), F32),
                dma((ng, 2)), dma((ng, 2)), dma((ng, 2)), dma((ng, 2)), dma((ng, 2)), dma((ng, 2)), dma((ng, 2)),
                dma((2,)), dma((2,)), dma((NP,)), dma((b,)), dma(()), pltpu.SemaphoreType.REGULAR,
            ],
            compiler_params=pltpu.CompilerParams(
                dimension_semantics=('arbitrary',), collective_id=0, has_side_effects=True,
                vmem_limit_bytes=67043328),
            cost_estimate=pl.CostEstimate(flops=flops, bytes_accessed=4 * q.size * 2, transcendentals=0),
        )(q, do, o, lse, k, v)
        return heads(dq), heads(dk), heads(dv)

    spec = P('data', 'cp')
    return jax.shard_map(local, mesh=mesh, in_specs=(spec, spec, spec, spec, spec, P('data', None, 'cp')),
                         out_specs=(spec, spec, spec), check_vma=False)
```

time: 1670 us -> 532 us (0.32)
  waiting for transfers between devices: 740 us -> 0 us
  matrix products: 579 us -> 0 us
  Pallas kernels: 0 us -> 485 us
  other arithmetic: 166 us -> 0 us
  local copies, waits for them, and re-layouts: 113 us -> 44.5 us
  starting transfers between devices: 48.9 us -> 0 us
    ppermute x14 -> x0, waiting for transfers between devices: 740 us -> none  [the longest x12 699 us: local(): kc, vc, dk, dv = (lax.ppermute(x, 'cp', perm) for x in (kc, vc, dk, dv))]
    dot_general x25 -> x0, matrix products: 579 us -> none  [the longest x5 153 us: _block(): dp = jnp.einsum('bhgqd,bhkd->bhgqk', do, v, preferred_element_type=F32)]
    pallas_call x0 -> x1, Pallas kernels: none -> 485 us  [local(): pl.pallas_call(functools.partial(_kernel, b, hkv, grp, scale), grid=(b +...]
    concatenate x4 -> x0, local copies, waits for them, and re-layouts: 82.2 us -> none  [the longest x3 82.1 us: _later(): return (jnp.concatenate([jnp.zeros_like(dq), dq], 3), dk, dv)]
    convert_element_type x2 -> x0, other arithmetic: 74.7 us -> none  [the longest x1 70.1 us: local(): jnp.transpose(dq * scale, (0, 3, 1, 2, 4)).astype(BF16).reshape(b, t, hq, d)]
    add x6 -> x0, other arithmetic: 63.4 us -> none  [local(): dq, dk, dv = (dq + dq_s, dk + dk_s, dv + dv_s)]
    ppermute x14 -> x0, starting transfers between devices: 48.9 us -> none  [the longest x12 41.4 us: local(): kc, vc, dk, dv = (lax.ppermute(x, 'cp', perm) for x in (kc, vc, dk, dv))]
    reduce_sum x1 -> x0, other arithmetic: 16.9 us -> none  [_prepare(): delta = jnp.sum(do.astype(F32) * o.astype(F32), axis=-1)]
  transfers between devices with their start and end apart: 14 -> 0, of which waited for: 7 -> 0; matrix products, arithmetic and copies ran while one was open for 41% -> 0% of each run, Pallas kernels for 0% -> 0%
where the time goes in v1:
time: 532 us; the launch traced here: 530 us
  Pallas kernels  485 us (91%)
  local copies, waits for them, and re-layouts  44.5 us (8%)
    pallas_call x1, Pallas kernels, local(): pl.pallas_call(functools.partial(_kernel, b, hkv, grp, scale), grid=(b +...  485 us
    unnamed x5, local copies, waits for them, and re-layouts  37.8 us

profile of v1, /device:TPU:0, one launch (start us, length us, event | category | flops | bytes accessed | tf_op | source)
XLA Modules:
  0.0 530.4 jit_solution(3828053473047860332)
XLA Ops:
  0.6 6.7 %copy_bitcast_fusion = (bf16[32,2,256,128]{3,2,1,0:T(8,128)(2,1)}, bf16[32,2,256,128]{3,2,1,0:T(8,128)(2,1)}) fusion(bf16[32,256,2,128]{3,2,1,0:T(2,128)(2,1)} %param.8, bf16[32,256,2,128]{3,2,1,0:T(2,128)(2,1)} %param.7), kind=kLoop, calls=%fused_computation | loop fusion | bytes 16777216 | tf_op jit(solution)/shard_map/transpose | solution.py:258
  7.3 485.2 %shard_map.85 = (bf16[32,12,256,128]{3,2,1,0:T(8,128)(2,1)}, bf16[32,2,256,128]{3,2,1,0:T(8,128)(2,1)}, bf16[32,2,256,128]{3,2,1,0:T(8,128)(2,1)}, f32[32,2,2,2,128,128]{5,4,3,2,1,0:T(8,128)}) custom-call(bf16[32,12,256,128]{3,2,1,0:T(8,128)(2,1)} %bitcast.14, bf16[32,12,256,128]{3,2,1,0:T(8,128)(2,1)} %bitcast.15, bf16[32,12,256,128]{3,2,1,0:T(8,128)(2,1)} %bitcast.16, ...), custom_call_target="tpu_custom_call" | custom-call | flops 72477573120 | bytes 100663296 | tf_op jit(solution)/shard_map/pallas_call | solution.py:268
  492.5 0.0 copy-start
  492.5 8.7 %copy.11 = bf16[32,256,2,128]{3,2,1,0:T(2,128)(2,1)} copy(bf16[32,256,2,128]{3,1,2,0:T(8,128)(2,1)} %bitcast.13) | data formatting | bytes 8388608
  501.3 0.0 copy-done
  501.3 6.4 %copy.12 = bf16[32,256,2,128]{3,2,1,0:T(2,128)(2,1)} copy(bf16[32,256,2,128]{3,1,2,0:T(8,128)(2,1)S(1)} %bitcast.12) | data formatting | bytes 8388608
  507.6 22.7 %copy.16 = bf16[32,256,12,128]{3,1,2,0:T(8,128)(2,1)} copy(bf16[32,256,12,128]{3,1,2,0:T(8,128)(2,1)} %bitcast.11) | data formatting | bytes 50331648
Async XLA Ops:
  492.5 8.7 %copy-start = (bf16[32,2,256,128]{3,2,1,0:T(8,128)(2,1)S(1)}, bf16[32,2,256,128]{3,2,1,0:T(8,128)(2,1)}, u32[]{:S(2)}) copy-start(bf16[32,2,256,128]{3,2,1,0:T(8,128)(2,1)} %get-tuple-element.8) | copy-start | bytes 12582916

commit v2 on v1

--- a/solution.py
+++ b/solution.py
@@ -15,6 +15,9 @@
 NP = 4
 LAG = 7
 NO = 8
+AHEAD = 3
+RS, R0 = 6, 2
+RLAG = 6
 
 OWN, PARTNER, PEER, DIAG = 0, 1, 2, 3
 
@@ -25,10 +28,10 @@
 
 def _kernel(nb, hkv, grp, scale,
             q_ref, do_ref, o_ref, lse_ref, k_hbm, v_hbm,
-            dq_ref, dk_ref, dv_ref, rl_hbm,
-            kl, vl, acc, dl, ps, osum, buf, qt, dot_, dqt, lse_s, del_s,
+            dq_ref, dk_hbm, dv_hbm, rl_hbm,
+            kl, vl, kd, acc, dl, ps, osum, buf, ret, rps, fin, stage, qt, dot_, dqt, lse_s, del_s,
             loc_sem, xs_sem, xr_sem, es_sem, er_sem, fs_sem, fr_sem,
-            ds_sem, dr_sem, ps_sem, pr_sem, buf_sem, credit):
+            ds_sem, dr_sem, ps_sem, pr_sem, buf_sem, os_sem, rs_sem, rr_sem, ts_sem, tr_sem, credit):
     i = pl.program_id(0)
     r = lax.axis_index('cp')
     chip = r // 2
@@ -56,14 +59,14 @@
         src, dst = kv(w)
         b = pl.ds(j * GB, GB)
         t = pl.ds(0, 2 * C if full else C)
-        return pltpu.make_async_remote_copy(src.at[b, :, t], dst.at[b, PARTNER, :, t], xs_sem.at[j, w], xr_sem.at[j, w],
+        return pltpu.make_async_remote_copy(src.at[b, t], dst.at[b, PARTNER, t], xs_sem.at[j, w], xr_sem.at[j, w],
                                             device_id={'cp': partner}, device_id_type=MESH)
 
     def fwd_copy(j, w, full):
         _, dst = kv(w)
         b = pl.ds(j * GB, GB)
         t = pl.ds(0, 2 * C if full else C)
-        return pltpu.make_async_remote_copy(dst.at[b, PARTNER, :, t], dst.at[b, DIAG, :, t], fs_sem.at[j, w], fr_sem.at[j, w],
+        return pltpu.make_async_remote_copy(dst.at[b, PARTNER, t], dst.at[b, DIAG, t], fs_sem.at[j, w], fr_sem.at[j, w],
                                             device_id={'cp': peer}, device_id_type=MESH)
 
     def part_copy(m):
@@ -76,6 +79,28 @@
         n = pl.ds(0, 2 if full else 1)
         return pltpu.make_async_remote_copy(ps.at[s, n], rl_hbm.at[m, n], ps_sem.at[s], pr_sem.at[m],
                                             device_id={'cp': partner}, device_id_type=MESH)
+
+    def ret_copy(m):
+        n = m // RS
+        return pltpu.make_async_remote_copy(osum.at[lax.rem(m, NO)], ret.at[n], rs_sem.at[lax.rem(n, 2)], rr_sem.at[n],
+                                            device_id={'cp': partner}, device_id_type=MESH)
+
+    def fin_copy(m, w):
+        dst = (dk_hbm, dv_hbm)[w]
+        return pltpu.make_async_remote_copy(fin.at[w], dst.at[m], ts_sem.at[w], tr_sem.at[m // RS, w],
+                                            device_id={'cp': partner}, device_id_type=MESH)
+
+    def out_copy(m, w):
+        dst = (dk_hbm, dv_hbm)[w]
+        return pltpu.make_async_copy(stage.at[w], dst.at[m], os_sem.at[w])
+
+    def results(dst, a, a_slot, b_, b_slot):
+        for sg in range(2):
+            for w in range(2):
+                x = [a[(*a_slot, sg, g, w)] + b_[(*b_slot, sg, g, w)] for g in range(hkv)]
+                if w == 0:
+                    x = [y * scale for y in x]
+                dst[w, pl.ds(sg * C, C)] = jnp.stack(x, axis=1).astype(BF16)
 
     def forward(j):
         for c, full in ((0, True), (1, False)):
@@ -95,7 +120,7 @@
         @pl.loop(0, ng)
         def _(j):
             for c, full in ((0, False), (1, True)):
-                @pl.when(chip == c)
+                @pl.when((chip == c) if c == 0 else ((chip == c) & (j < AHEAD)))
                 def _():
                     for w in range(2):
                         x_copy(j, w, full).start()
@@ -122,6 +147,11 @@
                     for w in range(2):
                         fwd_copy(j, w, full).wait_recv()
 
+        @pl.when((lax.rem(i, GB) == 0) & (chip == 1) & (j >= 1) & (j < ng - AHEAD + 1))
+        def _():
+            for w in range(2):
+                x_copy(j + AHEAD - 1, w, True).start()
+
         @pl.when((lax.rem(i, GB) == GB // 2) & (i < nb - GB))
         def _():
             forward(j + 1)
@@ -129,6 +159,9 @@
         acc[slot] = jnp.zeros(acc.shape[1:], F32)
         dqt[...] = jnp.zeros_like(dqt)
         row = lax.rem(i, 8)
+        for w in range(2):
+            for sec in range(4):
+                kd[w, sec] = jnp.transpose(kv(w)[1][b, sec], (1, 0, 2))
         for g in range(hkv):
             for hh in range(grp):
                 h = g * grp + hh
@@ -148,8 +181,8 @@
             keys = pl.ds(pl.multiple_of(half * C, C), C)
             toks = pl.ds(pl.multiple_of(qs * C, C), C)
             for g in range(hkv):
-                k = kl[b, sec, g, keys, :]
-                v = vl[b, sec, g, keys, :]
+                k = kd[0, sec, g, keys, :]
+                v = kd[1, sec, g, keys, :]
                 heads = pl.ds(g * grp, grp)
                 s = _dot(k, qt[qs, g])
                 p = jnp.exp(s * scale - lse_s[qs, g])
@@ -196,45 +229,99 @@
         copy.wait_send()
         copy.wait_recv()
         osum[lax.rem(m, NO)] = acc[s, pl.ds(0, 2)] + dl[s, pl.ds(0, 2)]
+        kept = (chip == 0) & (lax.rem(m, RS) == R0)
         for c, full in ((0, True), (1, False)):
-            @pl.when((chip == c) & (m >= NP))
+            @pl.when((chip == c) & (m >= NP) if c else (chip == c) & (m >= NP) & (lax.rem(m - NP + RS, RS) != R0))
             def _():
                 sum_copy(m - NP, full).wait_send()
-        ps[s4] = acc[s, pl.ds(2, 2)] + dl[s, pl.ds(2, 2)]
+
+        @pl.when(kept)
+        def _():
+            rps[...] = acc[s, pl.ds(2, 2)] + dl[s, pl.ds(2, 2)]
+
+        @pl.when(jnp.logical_not(kept))
+        def _():
+            ps[s4] = acc[s, pl.ds(2, 2)] + dl[s, pl.ds(2, 2)]
 
         @pl.when(m < nb - 2)
         def _():
             pl.semaphore_signal(credit, inc=1, device_id={'cp': peer}, device_id_type=MESH)
-        for c, full in ((0, True), (1, False)):
-            @pl.when(chip == c)
+
+        @pl.when((chip == 0) & (lax.rem(m, RS) != R0))
+        def _():
+            sum_copy(m, True).start()
+
+        @pl.when(chip == 1)
+        def _():
+            @pl.when(lax.rem(m, RS) == R0)
             def _():
-                sum_copy(m, full).start()
+                ret_copy(m).start()
+            sum_copy(m, False).start()
+
+    @pl.when((chip == 0) & (i >= RLAG) & (i < nb + RLAG) & (lax.rem(i - RLAG + RS, RS) == R0))
+    def _():
+        m = i - RLAG
+        ret_copy(m).wait_recv()
+
+        @pl.when(m >= RS)
+        def _():
+            for w in range(2):
+                fin_copy(m - RS, w).wait_send()
+        results(fin, rps, (), ret, (m // RS,))
+        for w in range(2):
+            fin_copy(m, w).start()
 
     @pl.when(i >= LAG)
     def _():
         m = i - LAG
-        for c, full in ((0, False), (1, True)):
-            @pl.when(chip == c)
-            def _():
-                sum_copy(m, full).wait_recv()
-                n = pl.ds(0, 2 if full else 1)
-                copy = pltpu.make_async_copy(rl_hbm.at[m, n], buf.at[n], buf_sem)
-                copy.start()
-                copy.wait()
-        so = lax.rem(m, NO)
-        for sg in range(2):
-            for g in range(hkv):
-                tok = pl.ds(sg * C, C)
-                dk_ref[0, g, tok, :] = ((osum[so, sg, g, 0] + buf[sg, g, 0]) * scale).astype(BF16)
-                dv_ref[0, g, tok, :] = (osum[so, sg, g, 1] + buf[sg, g, 1]).astype(BF16)
+        back = (chip == 1) & (lax.rem(m, RS) == R0)
+        before = (chip == 1) & (lax.rem(m - 1 + RS, RS) == R0)
+
+        @pl.when(back)
+        def _():
+            ret_copy(m).wait_send()
+
+        @pl.when((m >= 1) & jnp.logical_not(before))
+        def _():
+            for w in range(2):
+                out_copy(m - 1, w).wait()
+
+        @pl.when(jnp.logical_not(back))
+        def _():
+            for c, full in ((0, False), (1, True)):
+                @pl.when(chip == c)
+                def _():
+                    sum_copy(m, full).wait_recv()
+                    n = pl.ds(0, 2 if full else 1)
+                    copy = pltpu.make_async_copy(rl_hbm.at[m, n], buf.at[n], buf_sem)
+                    copy.start()
+                    copy.wait()
+            results(stage, osum, (lax.rem(m, NO),), buf, ())
+            for w in range(2):
+                out_copy(m, w).start()
 
     @pl.when(i == nb + LAG - 1)
     def _():
+        for w in range(2):
+            out_copy(nb - 1, w).wait()
         for c, full in ((0, True), (1, False)):
             @pl.when(chip == c)
             def _():
                 for m in range(nb - NP, nb):
-                    sum_copy(m, full).wait_send()
+                    if c == 1 or m % RS != R0:
+                        sum_copy(m, full).wait_send()
+        returned = range(R0, nb, RS)
+
+        @pl.when(chip == 0)
+        def _():
+            for w in range(2):
+                fin_copy(returned[-1], w).wait_send()
+
+        @pl.when(chip == 1)
+        def _():
+            for m in returned:
+                for w in range(2):
+                    fin_copy(m, w).wait_recv()
 
         @pl.loop(0, ng)
         def _(j):
@@ -248,6 +335,11 @@
                         fwd_copy(j, w, not full).wait_send()
 
 
+def _finish(*refs):
+    for src, dst in zip(refs[:3], refs[3:]):
+        dst[...] = src[...]
+
+
 def solution(mesh):
     def local(q, k, v, do, o, lse):
         b, t, hq, d = q.shape
@@ -255,49 +347,62 @@
         grp = hq // hkv
         scale = d ** -0.5
         ng = b // GB
+        nr = len(range(R0, b, RS))
+        assert (b - 1) % RS != R0 and RLAG <= RS
         heads = lambda x: jnp.transpose(x, (0, 2, 1, 3))
-        q, do, o, k, v = (heads(x) for x in (q, do, o, k, v))
+        q, do, o = (heads(x) for x in (q, do, o))
         lse = jnp.transpose(lse, (1, 0, 2))
 
         last = b - 1
         big = pl.BlockSpec((1, hq, t, d), lambda i: (jnp.minimum(i, last), 0, 0, 0))
-        out = pl.BlockSpec((1, hkv, t, d), lambda i: (jnp.maximum(i - LAG, 0), 0, 0, 0))
         anyspec = pl.BlockSpec(memory_space=pl.ANY)
         dma = pltpu.SemaphoreType.DMA
         flops = 9 * b * hq * 5 * 2 * C * C * d
+        shapes = [jax.ShapeDtypeStruct((b, hq, t, d), BF16),
+                  jax.ShapeDtypeStruct((b, t, hkv, d), BF16),
+                  jax.ShapeDtypeStruct((b, t, hkv, d), BF16)]
         dq, dk, dv, _ = pl.pallas_call(
             functools.partial(_kernel, b, hkv, grp, scale),
             grid=(b + LAG,),
             in_specs=[big, big, big,
                       pl.BlockSpec((hq, 8, t), lambda i: (0, jnp.minimum(i, last) // 8, 0)),
                       anyspec, anyspec],
-            out_specs=[big, out, out, anyspec],
-            out_shape=[jax.ShapeDtypeStruct((b, hq, t, d), BF16),
-                       jax.ShapeDtypeStruct((b, hkv, t, d), BF16),
-                       jax.ShapeDtypeStruct((b, hkv, t, d), BF16),
-                       jax.ShapeDtypeStruct((b, 2, hkv, 2, C, d), F32)],
+            out_specs=[big, anyspec, anyspec, anyspec],
+            out_shape=[*shapes, jax.ShapeDtypeStruct((b, 2, hkv, 2, C, d), F32)],
             scratch_shapes=[
-                pltpu.VMEM((b, 4, hkv, t, d), BF16),
-                pltpu.VMEM((b, 4, hkv, t, d), BF16),
+                pltpu.VMEM((b, 4, t, hkv, d), BF16),
+                pltpu.VMEM((b, 4, t, hkv, d), BF16),
+                pltpu.VMEM((2, 4, hkv, t, d), BF16),
                 pltpu.VMEM((2, 8, hkv, 2, C, d), F32),
                 pltpu.VMEM((2, 4, hkv, 2, C, d), F32),
                 pltpu.VMEM((NP, 2, hkv, 2, C, d), F32),
                 pltpu.VMEM((NO, 2, hkv, 2, C, d), F32),
                 pltpu.VMEM((2, hkv, 2, C, d), F32),
+                pltpu.VMEM((nr, 2, hkv, 2, C, d), F32),
+                pltpu.VMEM((2, hkv, 2, C, d), F32),
+                pltpu.VMEM((2, t, hkv, d), BF16),
+                pltpu.VMEM((2, t, hkv, d), BF16),
                 pltpu.VMEM((2, hkv, d, grp * C), BF16),
                 pltpu.VMEM((2, hkv, d, grp * C), BF16),
                 pltpu.VMEM((2, hkv, d, grp * C), F32),
                 pltpu.VMEM((2, hkv, 1, grp * C), F32),
                 pltpu.VMEM((2, hkv, 1, grp * C), F32),
                 dma((ng, 2)), dma((ng, 2)), dma((ng, 2)), dma((ng, 2)), dma((ng, 2)), dma((ng, 2)), dma((ng, 2)),
-                dma((2,)), dma((2,)), dma((NP,)), dma((b,)), dma(()), pltpu.SemaphoreType.REGULAR,
+                dma((2,)), dma((2,)), dma((NP,)), dma((b,)), dma(()),
+                dma((2,)), dma((2,)), dma((nr,)), dma((2,)), dma((nr, 2)), pltpu.SemaphoreType.REGULAR,
             ],
             compiler_params=pltpu.CompilerParams(
                 dimension_semantics=('arbitrary',), collective_id=0, has_side_effects=True,
                 vmem_limit_bytes=67043328),
             cost_estimate=pl.CostEstimate(flops=flops, bytes_accessed=4 * q.size * 2, transcendentals=0),
         )(q, do, o, lse, k, v)
-        return heads(dq), heads(dk), heads(dv)
+
+        two = [pl.BlockSpec((2, *x.shape[1:]), lambda i: (i, 0, 0, 0)) for x in shapes]
+        dq, dk, dv = pl.pallas_call(
+            _finish, grid=(b // 2,), in_specs=two, out_specs=two, out_shape=shapes,
+            compiler_params=pltpu.CompilerParams(dimension_semantics=('arbitrary',)),
+        )(dq, dk, dv)
+        return heads(dq), dk, dv
 
     spec = P('data', 'cp')
     return jax.shard_map(local, mesh=mesh, in_specs=(spec, spec, spec, spec, spec, P('data', None, 'cp')),

time: 532 us -> 466 us (0.88)
  local copies, waits for them, and re-layouts: 44.5 us -> 0 us
  Pallas kernels: 485 us -> 464 us
    pallas_call x1, Pallas kernels: 485 us -> 437 us  [local(): pl.pallas_call(functools.partial(_kernel, b, hkv, grp, scale), grid=(b +...]
    unnamed x5 -> x0, local copies, waits for them, and re-layouts: 37.8 us -> none
    pallas_call x0 -> x1, Pallas kernels: none -> 26.6 us  [local(): pl.pallas_call(_finish, grid=(b // 2,), in_specs=two, out_specs=two, out_...]
    transpose x1 -> x0, local copies, waits for them, and re-layouts: 6.68 us -> none  [local(): heads = lambda x: jnp.transpose(x, (0, 2, 1, 3))]
where the time goes in v2:
time: 466 us; the launch traced here: 464 us
  Pallas kernels  464 us (100%)
    pallas_call x1, Pallas kernels, local(): pl.pallas_call(functools.partial(_kernel, b, hkv, grp, scale), grid=(b +...  437 us
    pallas_call x1, Pallas kernels, local(): pl.pallas_call(_finish, grid=(b // 2,), in_specs=two, out_specs=two, out_...  26.6 us

profile of v2, /device:TPU:0, one launch (start us, length us, event | category | flops | bytes accessed | tf_op | source)
XLA Modules:
  0.0 464.2 jit_solution(17104210407230983132)
XLA Ops:
  0.6 436.9 %shard_map.85 = (bf16[32,12,256,128]{3,2,1,0:T(8,128)(2,1)}, bf16[32,256,2,128]{3,2,1,0:T(2,128)(2,1)}, bf16[32,256,2,128]{3,2,1,0:T(2,128)(2,1)}, f32[32,2,2,2,128,128]{5,4,3,2,1,0:T(8,128)}) custom-call(bf16[32,12,256,128]{3,2,1,0:T(8,128)(2,1)} %bitcast.5, bf16[32,12,256,128]{3,2,1,0:T(8,128)(2,1)} %bitcast.6, bf16[32,12,256,128]{3,2,1,0:T(8,128)(2,1)} %bitcast.7, ...), custom_call_target="tpu_custom_call" | custom-call | flops 72477573120 | bytes 100663296 | tf_op jit(solution)/shard_map/pallas_call | solution.py:364
  437.6 26.6 %shard_map.86 = (bf16[32,12,256,128]{3,2,1,0:T(8,128)(2,1)}, bf16[32,256,2,128]{3,2,1,0:T(2,128)(2,1)}, bf16[32,256,2,128]{3,2,1,0:T(2,128)(2,1)}) custom-call(bf16[32,12,256,128]{3,2,1,0:T(8,128)(2,1)} %get-tuple-element.9.refs_0_, bf16[32,256,2,128]{3,2,1,0:T(2,128)(2,1)} %get-tuple-element.10.refs_1_, bf16[32,256,2,128]{3,2,1,0:T(2,128)(2,1)} %get-tuple-element.11.refs_2_), custom_call_target="tpu_custom_call" | custom-call | tf_op jit(solution)/shard_map/pallas_call | solution.py:401

commit v3 on v2

--- a/solution.py
+++ b/solution.py
@@ -16,8 +16,9 @@
 LAG = 7
 NO = 8
 AHEAD = 3
-RS, R0 = 6, 2
+RS, R0 = 8, 2
 RLAG = 6
+NL = 3
 
 OWN, PARTNER, PEER, DIAG = 0, 1, 2, 3
 
@@ -28,10 +29,10 @@
 
 def _kernel(nb, hkv, grp, scale,
             q_ref, do_ref, o_ref, lse_ref, k_hbm, v_hbm,
-            dq_ref, dk_hbm, dv_hbm, rl_hbm,
+            dq_ref, dk_hbm, dv_hbm, rl_hbm, ol_hbm, pl_hbm,
             kl, vl, kd, acc, dl, ps, osum, buf, ret, rps, fin, stage, qt, dot_, dqt, lse_s, del_s,
             loc_sem, xs_sem, xr_sem, es_sem, er_sem, fs_sem, fr_sem,
-            ds_sem, dr_sem, ps_sem, pr_sem, buf_sem, os_sem, rs_sem, rr_sem, ts_sem, tr_sem, credit):
+            ds_sem, dr_sem, ps_sem, pr_sem, buf_sem, os_sem, rs_sem, rr_sem, ts_sem, tr_sem, tail_sem, credit):
     i = pl.program_id(0)
     r = lax.axis_index('cp')
     chip = r // 2
@@ -93,6 +94,11 @@
     def out_copy(m, w):
         dst = (dk_hbm, dv_hbm)[w]
         return pltpu.make_async_copy(stage.at[w], dst.at[m], os_sem.at[w])
+
+    def tail_copies(m):
+        n = m - (nb - NL)
+        return (pltpu.make_async_copy(osum.at[lax.rem(m, NO)], ol_hbm.at[n], tail_sem.at[n, 0]),
+                pltpu.make_async_copy(ps.at[lax.rem(m, NP)], pl_hbm.at[n], tail_sem.at[n, 1]))
 
     def results(dst, a, a_slot, b_, b_slot):
         for sg in range(2):
@@ -247,18 +253,23 @@
         def _():
             pl.semaphore_signal(credit, inc=1, device_id={'cp': peer}, device_id_type=MESH)
 
-        @pl.when((chip == 0) & (lax.rem(m, RS) != R0))
+        @pl.when(m >= nb - NL)
+        def _():
+            for copy in tail_copies(m):
+                copy.start()
+
+        @pl.when((chip == 0) & (lax.rem(m, RS) != R0) & (m < nb - NL))
         def _():
             sum_copy(m, True).start()
 
-        @pl.when(chip == 1)
+        @pl.when((chip == 1) & (m < nb - NL))
         def _():
             @pl.when(lax.rem(m, RS) == R0)
             def _():
                 ret_copy(m).start()
             sum_copy(m, False).start()
 
-    @pl.when((chip == 0) & (i >= RLAG) & (i < nb + RLAG) & (lax.rem(i - RLAG + RS, RS) == R0))
+    @pl.when((chip == 0) & (i >= RLAG) & (i < nb - NL + RLAG) & (lax.rem(i - RLAG + RS, RS) == R0))
     def _():
         m = i - RLAG
         ret_copy(m).wait_recv()
@@ -300,17 +311,20 @@
             for w in range(2):
                 out_copy(m, w).start()
 
-    @pl.when(i == nb + LAG - 1)
+    @pl.when(i == nb - NL + LAG - 1)
     def _():
         for w in range(2):
-            out_copy(nb - 1, w).wait()
+            out_copy(nb - NL - 1, w).wait()
         for c, full in ((0, True), (1, False)):
             @pl.when(chip == c)
             def _():
-                for m in range(nb - NP, nb):
+                for m in range(nb - NP, nb - NL):
                     if c == 1 or m % RS != R0:
                         sum_copy(m, full).wait_send()
-        returned = range(R0, nb, RS)
+        for m in range(nb - NL, nb):
+            for copy in tail_copies(m):
+                copy.wait()
+        returned = range(R0, nb - NL, RS)
 
         @pl.when(chip == 0)
         def _():
@@ -340,15 +354,28 @@
         dst[...] = src[...]
 
 
+def _last(scale, dk_in, dv_in, own_ref, got_ref, dk_ref, dv_ref):
+    n = pl.program_id(0)
+    hkv = own_ref.shape[2]
+    for sg in range(2):
+        for w, dst in enumerate((dk_ref, dv_ref)):
+            x = [own_ref[n, sg, g, w] + got_ref[n, sg, g, w] for g in range(hkv)]
+            if w == 0:
+                x = [y * scale for y in x]
+            dst[0, pl.ds(sg * C, C)] = jnp.stack(x, axis=1).astype(BF16)
+
+
 def solution(mesh):
+    swap = [(r, (r + 2) % 4) for r in range(4)]
+
     def local(q, k, v, do, o, lse):
         b, t, hq, d = q.shape
         hkv = k.shape[2]
         grp = hq // hkv
         scale = d ** -0.5
         ng = b // GB
-        nr = len(range(R0, b, RS))
-        assert (b - 1) % RS != R0 and RLAG <= RS
+        nr = len(range(R0, b - NL, RS))
+        assert (b - NL - 1) % RS != R0 and RLAG <= RS and NL <= NP
         heads = lambda x: jnp.transpose(x, (0, 2, 1, 3))
         q, do, o = (heads(x) for x in (q, do, o))
         lse = jnp.transpose(lse, (1, 0, 2))
@@ -361,14 +388,14 @@
         shapes = [jax.ShapeDtypeStruct((b, hq, t, d), BF16),
                   jax.ShapeDtypeStruct((b, t, hkv, d), BF16),
                   jax.ShapeDtypeStruct((b, t, hkv, d), BF16)]
-        dq, dk, dv, _ = pl.pallas_call(
+        dq, dk, dv, _, own, sums = pl.pallas_call(
             functools.partial(_kernel, b, hkv, grp, scale),
-            grid=(b + LAG,),
+            grid=(b - NL + LAG,),
             in_specs=[big, big, big,
                       pl.BlockSpec((hq, 8, t), lambda i: (0, jnp.minimum(i, last) // 8, 0)),
                       anyspec, anyspec],
-            out_specs=[big, anyspec, anyspec, anyspec],
-            out_shape=[*shapes, jax.ShapeDtypeStruct((b, 2, hkv, 2, C, d), F32)],
+            out_specs=[big, *[anyspec] * 5],
+            out_shape=[*shapes, *(jax.ShapeDtypeStruct((n, 2, hkv, 2, C, d), F32) for n in (b, NL, NL))],
             scratch_shapes=[
                 pltpu.VMEM((b, 4, t, hkv, d), BF16),
                 pltpu.VMEM((b, 4, t, hkv, d), BF16),
@@ -389,7 +416,7 @@
                 pltpu.VMEM((2, hkv, 1, grp * C), F32),
                 dma((ng, 2)), dma((ng, 2)), dma((ng, 2)), dma((ng, 2)), dma((ng, 2)), dma((ng, 2)), dma((ng, 2)),
                 dma((2,)), dma((2,)), dma((NP,)), dma((b,)), dma(()),
-                dma((2,)), dma((2,)), dma((nr,)), dma((2,)), dma((nr, 2)), pltpu.SemaphoreType.REGULAR,
+                dma((2,)), dma((2,)), dma((nr,)), dma((2,)), dma((nr, 2)), dma((NL, 2)), pltpu.SemaphoreType.REGULAR,
             ],
             compiler_params=pltpu.CompilerParams(
                 dimension_semantics=('arbitrary',), collective_id=0, has_side_effects=True,
@@ -397,11 +424,20 @@
             cost_estimate=pl.CostEstimate(flops=flops, bytes_accessed=4 * q.size * 2, transcendentals=0),
         )(q, do, o, lse, k, v)
 
+        got = lax.ppermute(sums, 'cp', swap)
         two = [pl.BlockSpec((2, *x.shape[1:]), lambda i: (i, 0, 0, 0)) for x in shapes]
         dq, dk, dv = pl.pallas_call(
             _finish, grid=(b // 2,), in_specs=two, out_specs=two, out_shape=shapes,
             compiler_params=pltpu.CompilerParams(dimension_semantics=('arbitrary',)),
+            cost_estimate=pl.CostEstimate(flops=10**8, bytes_accessed=4 * q.size, transcendentals=0),
         )(dq, dk, dv)
+        one = pl.BlockSpec(memory_space=pltpu.VMEM)
+        out = pl.BlockSpec((1, t, hkv, d), lambda i: (b - NL + i, 0, 0, 0))
+        dk, dv = pl.pallas_call(
+            functools.partial(_last, scale), grid=(NL,), in_specs=[anyspec, anyspec, one, one],
+            out_specs=[out, out], out_shape=shapes[1:], input_output_aliases={0: 0, 1: 1},
+            compiler_params=pltpu.CompilerParams(dimension_semantics=('arbitrary',)),
+        )(dk, dv, own, got)
         return heads(dq), dk, dv
 
     spec = P('data', 'cp')

time: 466 us -> 467 us (level)
  Pallas kernels: 464 us -> 452 us
  waiting for transfers between devices: 0 us -> 8.37 us
    pallas_call x1 -> x2, Pallas kernels: 437 us -> 426 us  [the longest x1 422 us: local(): pl.pallas_call(functools.partial(_kernel, b, hkv, grp, scale), grid=(b -...]
    ppermute x0 -> x1, waiting for transfers between devices: none -> 8.37 us  [local(): got = lax.ppermute(sums, 'cp', swap)]
  transfers between devices with their start and end apart: 0 -> 1, of which waited for: 0 -> 1; matrix products, arithmetic and copies ran while one was open for 0% -> 0% of each run, Pallas kernels for 0% -> 6%
where the time goes in v3:
time: 467 us; the launch traced here: 465 us
  Pallas kernels  452 us (97%)
  waiting for transfers between devices  8.37 us (2%)
    pallas_call x1, Pallas kernels, local(): pl.pallas_call(functools.partial(_kernel, b, hkv, grp, scale), grid=(b -...  422 us
    pallas_call x1, Pallas kernels, local(): pl.pallas_call(_finish, grid=(b // 2,), in_specs=two, out_specs=two, out_...  26.6 us
  transfers between devices with their start and end apart: 1, of which 1 were waited for; matrix products, arithmetic and copies ran while one was open for 0% of the time, Pallas kernels for 6%

profile of v3, /device:TPU:0, one launch (start us, length us, event | category | flops | bytes accessed | tf_op | source)
XLA Modules:
  0.0 465.2 jit_solution(2114667647346444266)
XLA Ops:
  0.6 421.7 %shard_map.85 = (bf16[32,12,256,128]{3,2,1,0:T(8,128)(2,1)}, bf16[32,256,2,128]{3,2,1,0:T(2,128)(2,1)}, bf16[32,256,2,128]{3,2,1,0:T(2,128)(2,1)}, f32[32,2,2,2,...) custom-call(bf16[32,12,256,128]{3,2,1,0:T(8,128)(2,1)} %bitcast.5, ...), custom_call_target="tpu_custom_call" | custom-call | flops 72477573120 | bytes 100663296 | tf_op jit(solution)/shard_map/pallas_call | solution.py:391
  422.3 2.6 collective-permute-start
  424.9 26.6 %shard_map.86 = (bf16[32,12,256,128]{3,2,1,0:T(8,128)(2,1)}, bf16[32,256,2,128]{3,2,1,0:T(2,128)(2,1)}, bf16[32,256,2,128]{3,2,1,0:T(2,128)(2,1)}) custom-call(bf16[32,12,256,128]{3,2,1,0:T(8,128)(2,1)} %get-tuple-element.13.refs_0_, bf16[32,256,2,128]{3,2,1,0:T(2,128)(2,1)} %get-tuple-element.14.refs_1_, bf16[32,256,2,128]{3,2,1,0:T(2,128)(2,1)} %get-tuple-element.15.refs_2_), custom_call_target="tpu_custom_call" | custom-call | flops 100000000 | bytes 50331648 | tf_op jit(solution)/shard_map/pallas_call | solution.py:429
  451.5 8.4 %collective-permute-done.got_ref = f32[3,2,2,2,128,128]{5,4,3,2,1,0:T(8,128)S(1)} collective-permute-done((f32[3,2,2,2,128,128]{5,4,3,2,1,0:T(8,128)}, f32[3,2,2,2,128,128]{5,4,3,2,1,0:T(8,128)S(1)}, u32[]{:S(2)}, u32[]{:S(2)}) %collective-permute-start) | collective-permute-done | bytes 1572896 | tf_op jit(solution)/shard_map/ppermute | solution.py:427
  459.9 0.0 copy-start
  459.9 1.2 copy-done
  461.0 4.1 shard_map.87
Async XLA Ops:
  422.3 37.6 %collective-permute-start = (f32[3,2,2,2,128,128]{5,4,3,2,1,0:T(8,128)}, f32[3,2,2,2,128,128]{5,4,3,2,1,0:T(8,128)S(1)}, u32[]{:S(2)}, u32[]{:S(2)}) collective-permute-start(f32[3,2,2,2,128,128]{5,4,3,2,1,0:T(8,128)} %get-tuple-element.20), channel_id=1, source_target_pairs={{0,2},{1,3},{2,0},{3,1},{4,6},{5,7},{6,4},{7,5}} | collective-permute-start | bytes 4718600 | tf_op jit(solution)/shard_map/ppermute | solution.py:427
  459.9 1.2 copy-start

commit v4 on v3

--- a/solution.py
+++ b/solution.py
@@ -13,7 +13,7 @@
 C = 128
 GB = 4
 NP = 4
-LAG = 7
+LAG = 8
 NO = 8
 AHEAD = 3
 RS, R0 = 8, 2
@@ -30,7 +30,7 @@
 def _kernel(nb, hkv, grp, scale,
             q_ref, do_ref, o_ref, lse_ref, k_hbm, v_hbm,
             dq_ref, dk_hbm, dv_hbm, rl_hbm, ol_hbm, pl_hbm,
-            kl, vl, kd, acc, dl, ps, osum, buf, ret, rps, fin, stage, qt, dot_, dqt, lse_s, del_s,
+            kl, vl, raw, acc, dl, ps, osum, buf, ret, rps, fin, stage, qt, dot_, dqt, lse_s, del_s,
             loc_sem, xs_sem, xr_sem, es_sem, er_sem, fs_sem, fr_sem,
             ds_sem, dr_sem, ps_sem, pr_sem, buf_sem, os_sem, rs_sem, rr_sem, ts_sem, tr_sem, tail_sem, credit):
     i = pl.program_id(0)
@@ -46,28 +46,27 @@
         return (k_hbm, kl) if which == 0 else (v_hbm, vl)
 
     def local_copy(j, w):
-        src, dst = kv(w)
+        n = lax.rem(j, 2)
+        return pltpu.make_async_copy(kv(w)[0].at[pl.ds(j * GB, GB)], raw.at[n, w], loc_sem.at[n, w])
+
+    def peer_copy(j, w):
+        _, dst = kv(w)
         b = pl.ds(j * GB, GB)
-        return pltpu.make_async_copy(src.at[b], dst.at[b, OWN], loc_sem.at[j, w])
-
-    def peer_copy(j, w):
-        src, dst = kv(w)
-        b = pl.ds(j * GB, GB)
-        return pltpu.make_async_remote_copy(src.at[b], dst.at[b, PEER], es_sem.at[j, w], er_sem.at[j, w],
+        return pltpu.make_async_remote_copy(dst.at[b, OWN], dst.at[b, PEER], es_sem.at[j, w], er_sem.at[j, w],
                                             device_id={'cp': peer}, device_id_type=MESH)
 
     def x_copy(j, w, full):
-        src, dst = kv(w)
+        _, dst = kv(w)
         b = pl.ds(j * GB, GB)
         t = pl.ds(0, 2 * C if full else C)
-        return pltpu.make_async_remote_copy(src.at[b, t], dst.at[b, PARTNER, t], xs_sem.at[j, w], xr_sem.at[j, w],
+        return pltpu.make_async_remote_copy(dst.at[b, OWN, :, t], dst.at[b, PARTNER, :, t], xs_sem.at[j, w], xr_sem.at[j, w],
                                             device_id={'cp': partner}, device_id_type=MESH)
 
     def fwd_copy(j, w, full):
         _, dst = kv(w)
         b = pl.ds(j * GB, GB)
         t = pl.ds(0, 2 * C if full else C)
-        return pltpu.make_async_remote_copy(dst.at[b, PARTNER, t], dst.at[b, DIAG, t], fs_sem.at[j, w], fr_sem.at[j, w],
+        return pltpu.make_async_remote_copy(dst.at[b, PARTNER, :, t], dst.at[b, DIAG, :, t], fs_sem.at[j, w], fr_sem.at[j, w],
                                             device_id={'cp': peer}, device_id_type=MESH)
 
     def part_copy(m):
@@ -94,6 +93,10 @@
     def out_copy(m, w):
         dst = (dk_hbm, dv_hbm)[w]
         return pltpu.make_async_copy(stage.at[w], dst.at[m], os_sem.at[w])
+
+    def buf_copy(m, full):
+        n = pl.ds(0, 2 if full else 1)
+        return pltpu.make_async_copy(rl_hbm.at[m, n], buf.at[n], buf_sem)
 
     def tail_copies(m):
         n = m - (nb - NL)
@@ -123,18 +126,42 @@
             pl.semaphore_signal(barrier, inc=1, device_id={'cp': other}, device_id_type=MESH)
         pl.semaphore_wait(barrier, 2)
 
+        for j in range(2):
+            for w in range(2):
+                local_copy(j, w).start()
+
         @pl.loop(0, ng)
         def _(j):
+            for w in range(2):
+                local_copy(j, w).wait()
+                for n in range(GB):
+                    kv(w)[1][j * GB + n, OWN] = jnp.transpose(raw[lax.rem(j, 2), w, n], (1, 0, 2))
             for c, full in ((0, False), (1, True)):
                 @pl.when((chip == c) if c == 0 else ((chip == c) & (j < AHEAD)))
                 def _():
                     for w in range(2):
                         x_copy(j, w, full).start()
             for w in range(2):
-                local_copy(j, w).start()
                 peer_copy(j, w).start()
+
+            @pl.when(j < ng - 2)
+            def _():
+                for w in range(2):
+                    local_copy(j + 2, w).start()
         buf[...] = jnp.zeros_like(buf)
         forward(0)
+
+    @pl.when(i >= LAG)
+    def _():
+        m = i - LAG
+
+        @pl.when((chip == 0) | (lax.rem(m, RS) != R0))
+        def _():
+            for c, full in ((0, False), (1, True)):
+                @pl.when(chip == c)
+                def _():
+                    sum_copy(m, full).wait_recv()
+                    buf_copy(m, full).start()
 
     @pl.when(i < nb)
     def _():
@@ -145,7 +172,6 @@
         @pl.when(lax.rem(i, GB) == 0)
         def _():
             for w in range(2):
-                local_copy(j, w).wait()
                 peer_copy(j, w).wait_recv()
             for c, full in ((0, True), (1, False)):
                 @pl.when(chip == c)
@@ -165,9 +191,6 @@
         acc[slot] = jnp.zeros(acc.shape[1:], F32)
         dqt[...] = jnp.zeros_like(dqt)
         row = lax.rem(i, 8)
-        for w in range(2):
-            for sec in range(4):
-                kd[w, sec] = jnp.transpose(kv(w)[1][b, sec], (1, 0, 2))
         for g in range(hkv):
             for hh in range(grp):
                 h = g * grp + hh
@@ -175,56 +198,56 @@
                 lse_row = lse_ref[h, pl.ds(row, 1), :]
                 for sg in range(2):
                     tok = pl.ds(sg * C, C)
-                    dob = do_ref[0, h, tok, :]
+                    do_t = do_ref[0, h, tok, :].T
                     qt[sg, g, :, lanes] = q_ref[0, h, tok, :].T
-                    dot_[sg, g, :, lanes] = dob.T
-                    prod = dob.astype(F32) * o_ref[0, h, tok, :].astype(F32)
-                    del_s[sg, g, :, lanes] = jnp.sum(prod.T, axis=0, keepdims=True)
+                    dot_[sg, g, :, lanes] = do_t
+                    prod = do_t.astype(F32) * o_ref[0, h, tok, :].T.astype(F32)
+                    del_s[sg, g, :, lanes] = jnp.sum(prod, axis=0, keepdims=True)
                     lse_s[sg, g, :, lanes] = lse_row[:, sg * C:(sg + 1) * C]
 
-        def pair(qs, ks, shift):
-            sec, half = ks // 2, lax.rem(ks, 2)
-            keys = pl.ds(pl.multiple_of(half * C, C), C)
+        def block(qs, kss, shifts):
             toks = pl.ds(pl.multiple_of(qs * C, C), C)
             for g in range(hkv):
-                k = kd[0, sec, g, keys, :]
-                v = kd[1, sec, g, keys, :]
+                def keys(src):
+                    x = [src[b, ks // 2, g, pl.ds(pl.multiple_of(lax.rem(ks, 2) * C, C), C), :] for ks in kss]
+                    return x[0] if len(x) == 1 else jnp.concatenate(x, axis=0)
+
+                k = keys(kl)
                 heads = pl.ds(g * grp, grp)
-                s = _dot(k, qt[qs, g])
-                p = jnp.exp(s * scale - lse_s[qs, g])
-                if shift is not None:
+                p = jnp.exp(_dot(k, qt[qs, g]) * scale - lse_s[qs, g])
+                if shifts is not None:
                     ki = lax.broadcasted_iota(jnp.int32, (C, rows), 0)
                     qi = lax.bitwise_and(lax.broadcasted_iota(jnp.int32, (C, rows), 1), C - 1)
-                    p = jnp.where(ki <= qi + shift, p, 0.0)
-                dp = _dot(v, dot_[qs, g])
-                ds = (p * (dp - del_s[qs, g])).astype(BF16)
-                acc[slot, ks, g, 1] += _dot(p.astype(BF16), do_ref[0, heads, toks, :].reshape(rows, C))
-                acc[slot, ks, g, 0] += _dot(ds, q_ref[0, heads, toks, :].reshape(rows, C))
+                    x = [jnp.where(ki <= qi + shift, p[n * C:(n + 1) * C], 0.0) for n, shift in enumerate(shifts)]
+                    p = x[0] if len(x) == 1 else jnp.concatenate(x, axis=0)
+                ds = (p * (_dot(keys(vl), dot_[qs, g]) - del_s[qs, g])).astype(BF16)
+                dv = _dot(p.astype(BF16), do_ref[0, heads, toks, :].reshape(rows, C))
+                dk = _dot(ds, q_ref[0, heads, toks, :].reshape(rows, C))
+                for n, ks in enumerate(kss):
+                    acc[slot, ks, g, 0] += dk[n * C:(n + 1) * C]
+                    acc[slot, ks, g, 1] += dv[n * C:(n + 1) * C]
                 dqt[qs, g] += _dot(k.T, ds)
-
-        @pl.loop(0, 3)
-        def _(t):
-            pair((t + 1) // 2, t // 2, C * lax.rem(t, 2))
 
         @pl.loop(0, 2)
         def _(t):
-            pair(1 - odd * (1 - t), 4 + t * (1 - odd), None)
-
-        @pl.loop(0, 4)
+            block(1 - t * odd, (4 * t * (1 - odd), 1 + t * (4 - odd)), (C * (1 - t * odd), C * t))
+
+        block(odd, (4 * odd,), (C * odd,))
+
+        @pl.loop(0, 2)
         def _(t):
-            u = (1 - chip) * t + chip * 2 * (t // 2)
-            pair((1 - chip) + chip * lax.rem(t, 2), 2 + lax.rem(u, 2) + 4 * (u // 2), None)
+            block((1 - chip) + chip * t, (2 + 4 * t * (1 - chip), (1 - chip) * (3 + 4 * t) + chip * 6), None)
+
+        @pl.when(i >= 2)
+        def _():
+            pl.semaphore_wait(credit, 1)
+        part_copy(i).start()
 
         for g in range(hkv):
             for hh in range(grp):
                 for sg in range(2):
                     x = dqt[sg, g, :, pl.ds(hh * C, C)].T
                     dq_ref[0, g * grp + hh, pl.ds(sg * C, C), :] = (x * scale).astype(BF16)
-
-        @pl.when(i >= 2)
-        def _():
-            pl.semaphore_wait(credit, 1)
-        part_copy(i).start()
 
     @pl.when((i >= 1) & (i <= nb))
     def _():
@@ -302,11 +325,7 @@
             for c, full in ((0, False), (1, True)):
                 @pl.when(chip == c)
                 def _():
-                    sum_copy(m, full).wait_recv()
-                    n = pl.ds(0, 2 if full else 1)
-                    copy = pltpu.make_async_copy(rl_hbm.at[m, n], buf.at[n], buf_sem)
-                    copy.start()
-                    copy.wait()
+                    buf_copy(m, full).wait()
             results(stage, osum, (lax.rem(m, NO),), buf, ())
             for w in range(2):
                 out_copy(m, w).start()
@@ -397,9 +416,9 @@
             out_specs=[big, *[anyspec] * 5],
             out_shape=[*shapes, *(jax.ShapeDtypeStruct((n, 2, hkv, 2, C, d), F32) for n in (b, NL, NL))],
             scratch_shapes=[
-                pltpu.VMEM((b, 4, t, hkv, d), BF16),
-                pltpu.VMEM((b, 4, t, hkv, d), BF16),
-                pltpu.VMEM((2, 4, hkv, t, d), BF16),
+                pltpu.VMEM((b, 4, hkv, t, d), BF16),
+                pltpu.VMEM((b, 4, hkv, t, d), BF16),
+                pltpu.VMEM((2, 2, GB, t, hkv, d), BF16),
                 pltpu.VMEM((2, 8, hkv, 2, C, d), F32),
                 pltpu.VMEM((2, 4, hkv, 2, C, d), F32),
                 pltpu.VMEM((NP, 2, hkv, 2, C, d), F32),
@@ -414,7 +433,7 @@
                 pltpu.VMEM((2, hkv, d, grp * C), F32),
                 pltpu.VMEM((2, hkv, 1, grp * C), F32),
                 pltpu.VMEM((2, hkv, 1, grp * C), F32),
-                dma((ng, 2)), dma((ng, 2)), dma((ng, 2)), dma((ng, 2)), dma((ng, 2)), dma((ng, 2)), dma((ng, 2)),
+                dma((2, 2)), dma((ng, 2)), dma((ng, 2)), dma((ng, 2)), dma((ng, 2)), dma((ng, 2)), dma((ng, 2)),
                 dma((2,)), dma((2,)), dma((NP,)), dma((b,)), dma(()),
                 dma((2,)), dma((2,)), dma((nr,)), dma((2,)), dma((nr, 2)), dma((NL, 2)), pltpu.SemaphoreType.REGULAR,
             ],

time: 467 us -> 445 us (0.953)
  Pallas kernels: 452 us -> 434 us
    pallas_call x1, Pallas kernels: 422 us -> 403 us  [local(): pl.pallas_call(functools.partial(_kernel, b, hkv, grp, scale), grid=(b -...]
where the time goes in v4:
time: 445 us
  Pallas kernels  434 us (98%)
  waiting for transfers between devices  7.06 us (2%)
    pallas_call x1, Pallas kernels, local(): pl.pallas_call(functools.partial(_kernel, b, hkv, grp, scale), grid=(b -...  403 us
    pallas_call x1, Pallas kernels, local(): pl.pallas_call(_finish, grid=(b // 2,), in_specs=two, out_specs=two, out_...  26.6 us
  transfers between devices with their start and end apart: 1, of which 1 were waited for; matrix products, arithmetic and copies ran while one was open for 0% of the time, Pallas kernels for 6%

profile of v4, /device:TPU:0, one launch (start us, length us, event | category | flops | bytes accessed | tf_op | source)
XLA Modules:
  0.0 444.9 jit_solution(17093084741843641014)
XLA Ops:
  0.6 402.8 %shard_map.85 = (bf16[32,12,256,128]{3,2,1,0:T(8,128)(2,1)}, bf16[32,256,2,128]{3,2,1,0:T(2,128)(2,1)}, bf16[32,256,2,128]{3,2,1,0:T(2,128)(2,1)}, f32[32,2,2,2,...) custom-call(bf16[32,12,256,128]{3,2,1,0:T(8,128)(2,1)} %bitcast.5, ...), custom_call_target="tpu_custom_call" | custom-call | flops 72477573120 | bytes 100663296 | tf_op jit(solution)/shard_map/pallas_call | solution.py:410
  403.5 2.5 collective-permute-start
  406.0 26.6 %shard_map.86 = (bf16[32,12,256,128]{3,2,1,0:T(8,128)(2,1)}, bf16[32,256,2,128]{3,2,1,0:T(2,128)(2,1)}, bf16[32,256,2,128]{3,2,1,0:T(2,128)(2,1)}) custom-call(bf16[32,12,256,128]{3,2,1,0:T(8,128)(2,1)} %get-tuple-element.13.refs_0_, bf16[32,256,2,128]{3,2,1,0:T(2,128)(2,1)} %get-tuple-element.14.refs_1_, bf16[32,256,2,128]{3,2,1,0:T(2,128)(2,1)} %get-tuple-element.15.refs_2_), custom_call_target="tpu_custom_call" | custom-call | flops 100000000 | bytes 50331648 | tf_op jit(solution)/shard_map/pallas_call | solution.py:448
  432.6 7.1 %collective-permute-done.got_ref = f32[3,2,2,2,128,128]{5,4,3,2,1,0:T(8,128)S(1)} collective-permute-done((f32[3,2,2,2,128,128]{5,4,3,2,1,0:T(8,128)}, f32[3,2,2,2,128,128]{5,4,3,2,1,0:T(8,128)S(1)}, u32[]{:S(2)}, u32[]{:S(2)}) %collective-permute-start) | collective-permute-done | bytes 1572896 | tf_op jit(solution)/shard_map/ppermute | solution.py:446
  439.6 0.0 copy-start
  439.6 1.2 copy-done
  440.8 4.1 shard_map.87
Async XLA Ops:
  403.5 36.2 %collective-permute-start = (f32[3,2,2,2,128,128]{5,4,3,2,1,0:T(8,128)}, f32[3,2,2,2,128,128]{5,4,3,2,1,0:T(8,128)S(1)}, u32[]{:S(2)}, u32[]{:S(2)}) collective-permute-start(f32[3,2,2,2,128,128]{5,4,3,2,1,0:T(8,128)} %get-tuple-element.20), channel_id=1, source_target_pairs={{0,2},{1,3},{2,0},{3,1},{4,6},{5,7},{6,4},{7,5}} | collective-permute-start | bytes 4718600 | tf_op jit(solution)/shard_map/ppermute | solution.py:446
  439.6 1.2 copy-start

commit v5 on v4

--- a/solution.py
+++ b/solution.py
@@ -16,8 +16,8 @@
 LAG = 8
 NO = 8
 AHEAD = 3
-RS, R0 = 8, 2
-RLAG = 6
+RS, R0 = 5, 1
+RLAG = 5
 NL = 3
 
 OWN, PARTNER, PEER, DIAG = 0, 1, 2, 3
@@ -41,6 +41,11 @@
     partner = lax.rem(r + 2, 4)
     ng = nb // GB
     rows = grp * C
+    first_late = nb - NL * (2 - chip)
+    first_kept = nb - NL * (1 + chip)
+
+    def returned(m):
+        return (lax.rem(m + RS, RS) == R0) & (m < nb - 2 * NL)
 
     def kv(which):
         return (k_hbm, kl) if which == 0 else (v_hbm, vl)
@@ -98,10 +103,22 @@
         n = pl.ds(0, 2 if full else 1)
         return pltpu.make_async_copy(rl_hbm.at[m, n], buf.at[n], buf_sem)
 
-    def tail_copies(m):
-        n = m - (nb - NL)
-        return (pltpu.make_async_copy(osum.at[lax.rem(m, NO)], ol_hbm.at[n], tail_sem.at[n, 0]),
-                pltpu.make_async_copy(ps.at[lax.rem(m, NP)], pl_hbm.at[n], tail_sem.at[n, 1]))
+    def late(m, act):
+        n = m - (nb - 2 * NL)
+        slot = lax.rem(m, NP)
+
+        @pl.when(m >= first_late)
+        def _():
+            act(pltpu.make_async_copy(osum.at[lax.rem(m, NO)], ol_hbm.at[n], tail_sem.at[n, 0]))
+
+        @pl.when((chip == 0) & (m >= first_kept))
+        def _():
+            act(pltpu.make_async_copy(ps.at[slot], pl_hbm.at[n - NL], tail_sem.at[n, 1]))
+
+        @pl.when((chip == 1) & (m >= first_kept))
+        def _():
+            one, at = pl.ds(0, 1), pl.ds(1 - n // NL, 1)
+            act(pltpu.make_async_copy(ps.at[slot, one], pl_hbm.at[lax.rem(n, NL), at], tail_sem.at[n, 1]))
 
     def results(dst, a, a_slot, b_, b_slot):
         for sg in range(2):
@@ -136,12 +153,10 @@
                 local_copy(j, w).wait()
                 for n in range(GB):
                     kv(w)[1][j * GB + n, OWN] = jnp.transpose(raw[lax.rem(j, 2), w, n], (1, 0, 2))
-            for c, full in ((0, False), (1, True)):
-                @pl.when((chip == c) if c == 0 else ((chip == c) & (j < AHEAD)))
-                def _():
-                    for w in range(2):
+                for c, full in ((0, False), (1, True)):
+                    @pl.when((chip == c) if c == 0 else ((chip == c) & (j < AHEAD)))
+                    def _():
                         x_copy(j, w, full).start()
-            for w in range(2):
                 peer_copy(j, w).start()
 
             @pl.when(j < ng - 2)
@@ -155,7 +170,7 @@
     def _():
         m = i - LAG
 
-        @pl.when((chip == 0) | (lax.rem(m, RS) != R0))
+        @pl.when((m < first_late) & ((chip == 0) | jnp.logical_not(returned(m))))
         def _():
             for c, full in ((0, False), (1, True)):
                 @pl.when(chip == c)
@@ -258,9 +273,10 @@
         copy.wait_send()
         copy.wait_recv()
         osum[lax.rem(m, NO)] = acc[s, pl.ds(0, 2)] + dl[s, pl.ds(0, 2)]
-        kept = (chip == 0) & (lax.rem(m, RS) == R0)
+        kept = (chip == 0) & returned(m)
         for c, full in ((0, True), (1, False)):
-            @pl.when((chip == c) & (m >= NP) if c else (chip == c) & (m >= NP) & (lax.rem(m - NP + RS, RS) != R0))
+            @pl.when((chip == c) & (m >= NP) &
+                     ((m - NP < first_kept) if c else jnp.logical_not(returned(m - NP))))
             def _():
                 sum_copy(m - NP, full).wait_send()
 
@@ -276,23 +292,26 @@
         def _():
             pl.semaphore_signal(credit, inc=1, device_id={'cp': peer}, device_id_type=MESH)
 
-        @pl.when(m >= nb - NL)
-        def _():
-            for copy in tail_copies(m):
-                copy.start()
-
-        @pl.when((chip == 0) & (lax.rem(m, RS) != R0) & (m < nb - NL))
+        @pl.when(m >= 1)
+        def _():
+            late(m - 1, lambda copy: copy.wait())
+        late(m, lambda copy: copy.start())
+
+        @pl.when((chip == 0) & jnp.logical_not(returned(m)) & (m < first_kept))
         def _():
             sum_copy(m, True).start()
 
-        @pl.when((chip == 1) & (m < nb - NL))
-        def _():
-            @pl.when(lax.rem(m, RS) == R0)
+        @pl.when(chip == 1)
+        def _():
+            @pl.when(returned(m))
             def _():
                 ret_copy(m).start()
-            sum_copy(m, False).start()
-
-    @pl.when((chip == 0) & (i >= RLAG) & (i < nb - NL + RLAG) & (lax.rem(i - RLAG + RS, RS) == R0))
+
+            @pl.when(m < first_kept)
+            def _():
+                sum_copy(m, False).start()
+
+    @pl.when((chip == 0) & (i >= RLAG) & returned(i - RLAG))
     def _():
         m = i - RLAG
         ret_copy(m).wait_recv()
@@ -308,19 +327,19 @@
     @pl.when(i >= LAG)
     def _():
         m = i - LAG
-        back = (chip == 1) & (lax.rem(m, RS) == R0)
-        before = (chip == 1) & (lax.rem(m - 1 + RS, RS) == R0)
+        back = (chip == 1) & returned(m)
+        before = (chip == 1) & returned(m - 1)
 
         @pl.when(back)
         def _():
             ret_copy(m).wait_send()
 
-        @pl.when((m >= 1) & jnp.logical_not(before))
+        @pl.when((m >= 1) & (m - 1 < first_late) & jnp.logical_not(before))
         def _():
             for w in range(2):
                 out_copy(m - 1, w).wait()
 
-        @pl.when(jnp.logical_not(back))
+        @pl.when((m < first_late) & jnp.logical_not(back))
         def _():
             for c, full in ((0, False), (1, True)):
                 @pl.when(chip == c)
@@ -332,27 +351,27 @@
 
     @pl.when(i == nb - NL + LAG - 1)
     def _():
-        for w in range(2):
-            out_copy(nb - NL - 1, w).wait()
-        for c, full in ((0, True), (1, False)):
-            @pl.when(chip == c)
-            def _():
-                for m in range(nb - NP, nb - NL):
-                    if c == 1 or m % RS != R0:
-                        sum_copy(m, full).wait_send()
-        for m in range(nb - NL, nb):
-            for copy in tail_copies(m):
-                copy.wait()
-        returned = range(R0, nb - NL, RS)
+        late(nb - 1, lambda copy: copy.wait())
+        all_returned = range(R0, nb - 2 * NL, RS)
+
+        @pl.when(chip == 1)
+        def _():
+            for w in range(2):
+                out_copy(nb - NL - 1, w).wait()
 
         @pl.when(chip == 0)
         def _():
-            for w in range(2):
-                fin_copy(returned[-1], w).wait_send()
+            for m in range(nb - NP, nb - NL):
+                sum_copy(m, True).wait_send()
+
+        @pl.when(chip == 0)
+        def _():
+            for w in range(2):
+                fin_copy(all_returned[-1], w).wait_send()
 
         @pl.when(chip == 1)
         def _():
-            for m in returned:
+            for m in all_returned:
                 for w in range(2):
                     fin_copy(m, w).wait_recv()
 
@@ -373,15 +392,37 @@
         dst[...] = src[...]
 
 
-def _last(scale, dk_in, dv_in, own_ref, got_ref, dk_ref, dv_ref):
-    n = pl.program_id(0)
+def _last(nb, scale, dk_in, dv_in, own_ref, got_ref, dk_hbm, dv_hbm, stage, sem):
+    chip = lax.axis_index('cp') // 2
     hkv = own_ref.shape[2]
-    for sg in range(2):
-        for w, dst in enumerate((dk_ref, dv_ref)):
-            x = [own_ref[n, sg, g, w] + got_ref[n, sg, g, w] for g in range(hkv)]
-            if w == 0:
-                x = [y * scale for y in x]
-            dst[0, pl.ds(sg * C, C)] = jnp.stack(x, axis=1).astype(BF16)
+    outs = (dk_hbm, dv_hbm)
+
+    def copies(n):
+        return [pltpu.make_async_copy(stage.at[n, w], outs[w].at[nb - 2 * NL + n], sem.at[n, w]) for w in range(2)]
+
+    def batch(n, terms):
+        for sg in range(2):
+            for w in range(2):
+                x = [own_ref[n, sg, g, w] for g in range(hkv)]
+                if terms[sg] is not None:
+                    x = [y + got_ref[(*terms[sg], g, w)] for g, y in enumerate(x)]
+                if w == 0:
+                    x = [y * scale for y in x]
+                stage[n, w, pl.ds(sg * C, C)] = jnp.stack(x, axis=1).astype(BF16)
+        for copy in copies(n):
+            copy.start()
+
+    for c in range(2):
+        @pl.when(chip == c)
+        def _():
+            for n in range(NL * c, 2 * NL):
+                if n < NL:
+                    batch(n, ((n, 1), None))
+                else:
+                    batch(n, ((n - NL, 0), (n - NL, 1) if c else None))
+            for n in range(NL * c, 2 * NL):
+                for copy in copies(n):
+                    copy.wait()
 
 
 def solution(mesh):
@@ -393,8 +434,8 @@
         grp = hq // hkv
         scale = d ** -0.5
         ng = b // GB
-        nr = len(range(R0, b - NL, RS))
-        assert (b - NL - 1) % RS != R0 and RLAG <= RS and NL <= NP
+        nr = len(range(R0, b - 2 * NL, RS))
+        assert RLAG <= RS and NL <= NP and 2 * NL <= NO
         heads = lambda x: jnp.transpose(x, (0, 2, 1, 3))
         q, do, o = (heads(x) for x in (q, do, o))
         lse = jnp.transpose(lse, (1, 0, 2))
@@ -414,7 +455,7 @@
                       pl.BlockSpec((hq, 8, t), lambda i: (0, jnp.minimum(i, last) // 8, 0)),
                       anyspec, anyspec],
             out_specs=[big, *[anyspec] * 5],
-            out_shape=[*shapes, *(jax.ShapeDtypeStruct((n, 2, hkv, 2, C, d), F32) for n in (b, NL, NL))],
+            out_shape=[*shapes, *(jax.ShapeDtypeStruct((n, 2, hkv, 2, C, d), F32) for n in (b, 2 * NL, NL))],
             scratch_shapes=[
                 pltpu.VMEM((b, 4, hkv, t, d), BF16),
                 pltpu.VMEM((b, 4, hkv, t, d), BF16),
@@ -435,7 +476,7 @@
                 pltpu.VMEM((2, hkv, 1, grp * C), F32),
                 dma((2, 2)), dma((ng, 2)), dma((ng, 2)), dma((ng, 2)), dma((ng, 2)), dma((ng, 2)), dma((ng, 2)),
                 dma((2,)), dma((2,)), dma((NP,)), dma((b,)), dma(()),
-                dma((2,)), dma((2,)), dma((nr,)), dma((2,)), dma((nr, 2)), dma((NL, 2)), pltpu.SemaphoreType.REGULAR,
+                dma((2,)), dma((2,)), dma((nr,)), dma((2,)), dma((nr, 2)), dma((2 * NL, 2)), pltpu.SemaphoreType.REGULAR,
             ],
             compiler_params=pltpu.CompilerParams(
                 dimension_semantics=('arbitrary',), collective_id=0, has_side_effects=True,
@@ -451,11 +492,10 @@
             cost_estimate=pl.CostEstimate(flops=10**8, bytes_accessed=4 * q.size, transcendentals=0),
         )(dq, dk, dv)
         one = pl.BlockSpec(memory_space=pltpu.VMEM)
-        out = pl.BlockSpec((1, t, hkv, d), lambda i: (b - NL + i, 0, 0, 0))
         dk, dv = pl.pallas_call(
-            functools.partial(_last, scale), grid=(NL,), in_specs=[anyspec, anyspec, one, one],
-            out_specs=[out, out], out_shape=shapes[1:], input_output_aliases={0: 0, 1: 1},
-            compiler_params=pltpu.CompilerParams(dimension_semantics=('arbitrary',)),
+            functools.partial(_last, b, scale), in_specs=[anyspec, anyspec, one, one],
+            out_specs=[anyspec, anyspec], out_shape=shapes[1:], input_output_aliases={0: 0, 1: 1},
+            scratch_shapes=[pltpu.VMEM((2 * NL, 2, t, hkv, d), BF16), dma((2 * NL, 2))],
         )(dk, dv, own, got)
         return heads(dq), dk, dv
 

time: 445 us -> 461 us (1.036)
  Pallas kernels: 434 us -> 441 us
  starting transfers between devices: 2.52 us -> 9.28 us
    ppermute x1, starting transfers between devices: 2.52 us -> 9.28 us  [local(): got = lax.ppermute(sums, 'cp', swap)]
    pallas_call x1, Pallas kernels: 403 us -> 409 us  [local(): pl.pallas_call(functools.partial(_kernel, b, hkv, grp, scale), grid=(b -...]
where the time goes in v5:
time: 461 us
  Pallas kernels  441 us (96%)
  starting transfers between devices  9.28 us (2%)
  waiting for transfers between devices  8.35 us (2%)
    pallas_call x1, Pallas kernels, local(): pl.pallas_call(functools.partial(_kernel, b, hkv, grp, scale), grid=(b -...  409 us
    pallas_call x1, Pallas kernels, local(): pl.pallas_call(_finish, grid=(b // 2,), in_specs=two, out_specs=two, out_...  26.6 us
    ppermute x1, starting transfers between devices, local(): got = lax.ppermute(sums, 'cp', swap)  9.28 us
  transfers between devices with their start and end apart: 1, of which 1 were waited for; matrix products, arithmetic and copies ran while one was open for 0% of the time, Pallas kernels for 6%

profile of v5, /device:TPU:0, one launch (start us, length us, event | category | flops | bytes accessed | tf_op | source)
XLA Modules:
  0.0 460.8 jit_solution(17419521032724051671)
XLA Ops:
  0.6 409.0 %shard_map.85 = (bf16[32,12,256,128]{3,2,1,0:T(8,128)(2,1)}, bf16[32,256,2,128]{3,2,1,0:T(2,128)(2,1)}, bf16[32,256,2,128]{3,2,1,0:T(2,128)(2,1)}, f32[32,2,2,2,...) custom-call(bf16[32,12,256,128]{3,2,1,0:T(8,128)(2,1)} %bitcast.5, ...), custom_call_target="tpu_custom_call" | custom-call | flops 72477573120 | bytes 100663296 | tf_op jit(solution)/shard_map/pallas_call | solution.py:451
  409.6 9.3 %collective-permute-start = (f32[3,2,2,2,128,128]{5,4,3,2,1,0:T(8,128)}, f32[3,2,2,2,128,128]{5,4,3,2,1,0:T(8,128)S(1)}, u32[]{:S(2)}, u32[]{:S(2)}) collective-permute-start(f32[3,2,2,2,128,128]{5,4,3,2,1,0:T(8,128)} %get-tuple-element.20), channel_id=1, source_target_pairs={{0,2},{1,3},{2,0},{3,1},{4,6},{5,7},{6,4},{7,5}} | collective-permute-start | bytes 4718600 | tf_op jit(solution)/shard_map/ppermute | solution.py:487
  418.9 26.6 %shard_map.86 = (bf16[32,12,256,128]{3,2,1,0:T(8,128)(2,1)}, bf16[32,256,2,128]{3,2,1,0:T(2,128)(2,1)}, bf16[32,256,2,128]{3,2,1,0:T(2,128)(2,1)}) custom-call(bf16[32,12,256,128]{3,2,1,0:T(8,128)(2,1)} %get-tuple-element.13.refs_0_, bf16[32,256,2,128]{3,2,1,0:T(2,128)(2,1)} %get-tuple-element.14.refs_1_, bf16[32,256,2,128]{3,2,1,0:T(2,128)(2,1)} %get-tuple-element.15.refs_2_), custom_call_target="tpu_custom_call" | custom-call | flops 100000000 | bytes 50331648 | tf_op jit(solution)/shard_map/pallas_call | solution.py:489
  445.5 8.3 %collective-permute-done.got_ref = f32[3,2,2,2,128,128]{5,4,3,2,1,0:T(8,128)S(1)} collective-permute-done((f32[3,2,2,2,128,128]{5,4,3,2,1,0:T(8,128)}, f32[3,2,2,2,128,128]{5,4,3,2,1,0:T(8,128)S(1)}, u32[]{:S(2)}, u32[]{:S(2)}) %collective-permute-start) | collective-permute-done | bytes 1572896 | tf_op jit(solution)/shard_map/ppermute | solution.py:487
  453.8 0.0 copy-start
  453.8 1.2 copy-done
  455.0 5.8 %shard_map.87 = (bf16[32,256,2,128]{3,2,1,0:T(2,128)(2,1)}, bf16[32,256,2,128]{3,2,1,0:T(2,128)(2,1)}) custom-call(bf16[32,256,2,128]{3,2,1,0:T(2,128)(2,1)} %get-tuple-element.17.dk_in, bf16[32,256,2,128]{3,2,1,0:T(2,128)(2,1)} %get-tuple-element.18.dv_in, ...), custom_call_target="tpu_custom_call", output_to_operand_aliasing={{0}: (0, {}), {1}: (1, {})} | custom-call | tf_op jit(solution)/shard_map/pallas_call | solution.py:495
Async XLA Ops:
  409.6 44.2 %collective-permute-start = (f32[3,2,2,2,128,128]{5,4,3,2,1,0:T(8,128)}, f32[3,2,2,2,128,128]{5,4,3,2,1,0:T(8,128)S(1)}, u32[]{:S(2)}, u32[]{:S(2)}) collective-permute-start(f32[3,2,2,2,128,128]{5,4,3,2,1,0:T(8,128)} %get-tuple-element.20), channel_id=1, source_target_pairs={{0,2},{1,3},{2,0},{3,1},{4,6},{5,7},{6,4},{7,5}} | collective-permute-start | bytes 4718600 | tf_op jit(solution)/shard_map/ppermute | solution.py:487
  453.8 1.2 copy-start

commit v6 on v5

--- a/solution.py
+++ b/solution.py
@@ -13,11 +13,11 @@
 C = 128
 GB = 4
 NP = 4
-LAG = 8
-NO = 8
+LAG = 11
+NO = 11
 AHEAD = 3
 RS, R0 = 5, 1
-RLAG = 5
+RLAG = 10
 NL = 3
 
 OWN, PARTNER, PEER, DIAG = 0, 1, 2, 3
@@ -51,8 +51,7 @@
         return (k_hbm, kl) if which == 0 else (v_hbm, vl)
 
     def local_copy(j, w):
-        n = lax.rem(j, 2)
-        return pltpu.make_async_copy(kv(w)[0].at[pl.ds(j * GB, GB)], raw.at[n, w], loc_sem.at[n, w])
+        return pltpu.make_async_copy(kv(w)[0].at[pl.ds(j * GB, GB)], raw.at[w], loc_sem.at[w])
 
     def peer_copy(j, w):
         _, dst = kv(w)
@@ -87,7 +86,7 @@
 
     def ret_copy(m):
         n = m // RS
-        return pltpu.make_async_remote_copy(osum.at[lax.rem(m, NO)], ret.at[n], rs_sem.at[lax.rem(n, 2)], rr_sem.at[n],
+        return pltpu.make_async_remote_copy(osum.at[lax.rem(m, NO)], ret.at[n], rs_sem.at[lax.rem(n, 3)], rr_sem.at[n],
                                             device_id={'cp': partner}, device_id_type=MESH)
 
     def fin_copy(m, w):
@@ -143,26 +142,25 @@
             pl.semaphore_signal(barrier, inc=1, device_id={'cp': other}, device_id_type=MESH)
         pl.semaphore_wait(barrier, 2)
 
-        for j in range(2):
-            for w in range(2):
-                local_copy(j, w).start()
+        for w in range(2):
+            local_copy(0, w).start()
 
         @pl.loop(0, ng)
         def _(j):
             for w in range(2):
                 local_copy(j, w).wait()
                 for n in range(GB):
-                    kv(w)[1][j * GB + n, OWN] = jnp.transpose(raw[lax.rem(j, 2), w, n], (1, 0, 2))
+                    kv(w)[1][j * GB + n, OWN] = jnp.transpose(raw[w, n], (1, 0, 2))
+
+                @pl.when(j < ng - 1)
+                def _():
+                    local_copy(j + 1, w).start()
                 for c, full in ((0, False), (1, True)):
                     @pl.when((chip == c) if c == 0 else ((chip == c) & (j < AHEAD)))
                     def _():
                         x_copy(j, w, full).start()
                 peer_copy(j, w).start()
 
-            @pl.when(j < ng - 2)
-            def _():
-                for w in range(2):
-                    local_copy(j + 2, w).start()
         buf[...] = jnp.zeros_like(buf)
         forward(0)
 
@@ -282,7 +280,7 @@
 
         @pl.when(kept)
         def _():
-            rps[...] = acc[s, pl.ds(2, 2)] + dl[s, pl.ds(2, 2)]
+            rps[lax.rem(m // RS, 2)] = acc[s, pl.ds(2, 2)] + dl[s, pl.ds(2, 2)]
 
         @pl.when(jnp.logical_not(kept))
         def _():
@@ -320,7 +318,7 @@
         def _():
             for w in range(2):
                 fin_copy(m - RS, w).wait_send()
-        results(fin, rps, (), ret, (m // RS,))
+        results(fin, rps, (lax.rem(m // RS, 2),), ret, (m // RS,))
         for w in range(2):
             fin_copy(m, w).start()
 
@@ -435,7 +433,7 @@
         scale = d ** -0.5
         ng = b // GB
         nr = len(range(R0, b - 2 * NL, RS))
-        assert RLAG <= RS and NL <= NP and 2 * NL <= NO
+        assert RLAG <= 2 * RS and LAG <= NO and LAG < 3 * RS and NL <= NP and 2 * NL <= NO
         heads = lambda x: jnp.transpose(x, (0, 2, 1, 3))
         q, do, o = (heads(x) for x in (q, do, o))
         lse = jnp.transpose(lse, (1, 0, 2))
@@ -459,14 +457,14 @@
             scratch_shapes=[
                 pltpu.VMEM((b, 4, hkv, t, d), BF16),
                 pltpu.VMEM((b, 4, hkv, t, d), BF16),
-                pltpu.VMEM((2, 2, GB, t, hkv, d), BF16),
+                pltpu.VMEM((2, GB, t, hkv, d), BF16),
                 pltpu.VMEM((2, 8, hkv, 2, C, d), F32),
                 pltpu.VMEM((2, 4, hkv, 2, C, d), F32),
                 pltpu.VMEM((NP, 2, hkv, 2, C, d), F32),
                 pltpu.VMEM((NO, 2, hkv, 2, C, d), F32),
                 pltpu.VMEM((2, hkv, 2, C, d), F32),
                 pltpu.VMEM((nr, 2, hkv, 2, C, d), F32),
-                pltpu.VMEM((2, hkv, 2, C, d), F32),
+                pltpu.VMEM((2, 2, hkv, 2, C, d), F32),
                 pltpu.VMEM((2, t, hkv, d), BF16),
                 pltpu.VMEM((2, t, hkv, d), BF16),
                 pltpu.VMEM((2, hkv, d, grp * C), BF16),
@@ -474,9 +472,9 @@
                 pltpu.VMEM((2, hkv, d, grp * C), F32),
                 pltpu.VMEM((2, hkv, 1, grp * C), F32),
                 pltpu.VMEM((2, hkv, 1, grp * C), F32),
-                dma((2, 2)), dma((ng, 2)), dma((ng, 2)), dma((ng, 2)), dma((ng, 2)), dma((ng, 2)), dma((ng, 2)),
+                dma((2,)), dma((ng, 2)), dma((ng, 2)), dma((ng, 2)), dma((ng, 2)), dma((ng, 2)), dma((ng, 2)),
                 dma((2,)), dma((2,)), dma((NP,)), dma((b,)), dma(()),
-                dma((2,)), dma((2,)), dma((nr,)), dma((2,)), dma((nr, 2)), dma((2 * NL, 2)), pltpu.SemaphoreType.REGULAR,
+                dma((2,)), dma((3,)), dma((nr,)), dma((2,)), dma((nr, 2)), dma((2 * NL, 2)), pltpu.SemaphoreType.REGULAR,
             ],
             compiler_params=pltpu.CompilerParams(
                 dimension_semantics=('arbitrary',), collective_id=0, has_side_effects=True,

time: 461 us -> 466 us (1.011)
  starting transfers between devices: 9.28 us -> 17.3 us
    ppermute x1, starting transfers between devices: 9.28 us -> 17.3 us  [local(): got = lax.ppermute(sums, 'cp', swap)]
where the time goes in v6:
time: 466 us; the launch traced here: 465 us
  Pallas kernels  438 us (94%)
  starting transfers between devices  17.3 us (4%)
  waiting for transfers between devices  8.35 us (2%)
    pallas_call x1, Pallas kernels, local(): pl.pallas_call(functools.partial(_kernel, b, hkv, grp, scale), grid=(b -...  406 us
    pallas_call x1, Pallas kernels, local(): pl.pallas_call(_finish, grid=(b // 2,), in_specs=two, out_specs=two, out_...  26.6 us
    ppermute x1, starting transfers between devices, local(): got = lax.ppermute(sums, 'cp', swap)  17.3 us
  transfers between devices with their start and end apart: 1, of which 1 were waited for; matrix products, arithmetic and copies ran while one was open for 0% of the time, Pallas kernels for 6%

profile of v6, /device:TPU:0, one launch (start us, length us, event | category | flops | bytes accessed | tf_op | source)
XLA Modules:
  0.0 465.4 jit_solution(17073113884407727879)
XLA Ops:
  0.6 405.6 %shard_map.85 = (bf16[32,12,256,128]{3,2,1,0:T(8,128)(2,1)}, bf16[32,256,2,128]{3,2,1,0:T(2,128)(2,1)}, bf16[32,256,2,128]{3,2,1,0:T(2,128)(2,1)}, f32[32,2,2,2,...) custom-call(bf16[32,12,256,128]{3,2,1,0:T(8,128)(2,1)} %bitcast.5, ...), custom_call_target="tpu_custom_call" | custom-call | flops 72477573120 | bytes 100663296 | tf_op jit(solution)/shard_map/pallas_call | solution.py:449
  406.2 17.3 %collective-permute-start = (f32[3,2,2,2,128,128]{5,4,3,2,1,0:T(8,128)}, f32[3,2,2,2,128,128]{5,4,3,2,1,0:T(8,128)S(1)}, u32[]{:S(2)}, u32[]{:S(2)}) collective-permute-start(f32[3,2,2,2,128,128]{5,4,3,2,1,0:T(8,128)} %get-tuple-element.20), channel_id=1, source_target_pairs={{0,2},{1,3},{2,0},{3,1},{4,6},{5,7},{6,4},{7,5}} | collective-permute-start | bytes 4718600 | tf_op jit(solution)/shard_map/ppermute | solution.py:485
  423.5 26.6 %shard_map.86 = (bf16[32,12,256,128]{3,2,1,0:T(8,128)(2,1)}, bf16[32,256,2,128]{3,2,1,0:T(2,128)(2,1)}, bf16[32,256,2,128]{3,2,1,0:T(2,128)(2,1)}) custom-call(bf16[32,12,256,128]{3,2,1,0:T(8,128)(2,1)} %get-tuple-element.13.refs_0_, bf16[32,256,2,128]{3,2,1,0:T(2,128)(2,1)} %get-tuple-element.14.refs_1_, bf16[32,256,2,128]{3,2,1,0:T(2,128)(2,1)} %get-tuple-element.15.refs_2_), custom_call_target="tpu_custom_call" | custom-call | flops 100000000 | bytes 50331648 | tf_op jit(solution)/shard_map/pallas_call | solution.py:487
  450.1 8.3 %collective-permute-done.got_ref = f32[3,2,2,2,128,128]{5,4,3,2,1,0:T(8,128)S(1)} collective-permute-done((f32[3,2,2,2,128,128]{5,4,3,2,1,0:T(8,128)}, f32[3,2,2,2,128,128]{5,4,3,2,1,0:T(8,128)S(1)}, u32[]{:S(2)}, u32[]{:S(2)}) %collective-permute-start) | collective-permute-done | bytes 1572896 | tf_op jit(solution)/shard_map/ppermute | solution.py:485
  458.4 0.0 copy-start
  458.4 1.2 copy-done
  459.6 5.8 %shard_map.87 = (bf16[32,256,2,128]{3,2,1,0:T(2,128)(2,1)}, bf16[32,256,2,128]{3,2,1,0:T(2,128)(2,1)}) custom-call(bf16[32,256,2,128]{3,2,1,0:T(2,128)(2,1)} %get-tuple-element.17.dk_in, bf16[32,256,2,128]{3,2,1,0:T(2,128)(2,1)} %get-tuple-element.18.dv_in, ...), custom_call_target="tpu_custom_call", output_to_operand_aliasing={{0}: (0, {}), {1}: (1, {})} | custom-call | tf_op jit(solution)/shard_map/pallas_call | solution.py:493
Async XLA Ops:
  406.2 52.2 %collective-permute-start = (f32[3,2,2,2,128,128]{5,4,3,2,1,0:T(8,128)}, f32[3,2,2,2,128,128]{5,4,3,2,1,0:T(8,128)S(1)}, u32[]{:S(2)}, u32[]{:S(2)}) collective-permute-start(f32[3,2,2,2,128,128]{5,4,3,2,1,0:T(8,128)} %get-tuple-element.20), channel_id=1, source_target_pairs={{0,2},{1,3},{2,0},{3,1},{4,6},{5,7},{6,4},{7,5}} | collective-permute-start | bytes 4718600 | tf_op jit(solution)/shard_map/ppermute | solution.py:485
  458.4 1.2 copy-start
